TPU v7x, 32 devices: a whole 2x2x4 slice. The times are simulated.
32 devices in a mesh: seq: 8 (over z, y), vocab: 4 (over x, core).
Axes of the slice: x: 2, y: 2, z: 4, core: 2. Of those that a mesh axis runs over, the one named last changes fastest.
Arguments:
- hidden: bfloat16 [768, 3584], P('seq', 'vocab'), may hold values from -40 to 40
- lm_head: bfloat16 [3584, 152064], P(None, ('seq', 'vocab')), may hold values from -1 to 1
- positions: int32 [768], replicated, may hold values from 0 to 767, as said below
- vocab_limits: int32 [768], replicated, may hold values from 76032 to 152064
- loss_mask: int32 [768], P('seq'), may hold values 0 or 1
Outputs:
- token_entropy: float32 [768], P('seq')
- mean_entropy: float32 [], replicated
Inputs may be any that keep to these rules, and one draw needn't show every extreme that they name: A permutation of the positions 0 to 767: the response is cut into 16 blocks of 48 consecutive positions; rows i * 96 to i * 96 + 96 // 2 - 1 hold the positions of block i, the next 48 rows those of block 15 - i, in any order within a block.
All inputs are finite; a program needn't handle non-finite values. No bound on the sum of `loss_mask` on one device may be relied on, other than what follows from the above.
Results may differ from a plain program's by a relative error of at most 0.0003.
Values may be sent and summed in bfloat16 or wider, within the bound.
No kernel may reach another device: no remote copies, remote signals or barrier semaphores. Data moves between devices by JAX's collectives and lax.ppermute only.
A program may use at most 128 MiB of HBM per device.

v0:
```python
import jax
import jax.numpy as jnp
from jax import lax
from jax.sharding import PartitionSpec as P

masked_value = -1e30


def row_stats(logits, row_limits, first_column):
    columns = first_column + lax.iota(jnp.int32, logits.shape[1])
    allowed = columns[None, :] < row_limits[:, None]
    row_peak = jnp.max(jnp.where(allowed, logits, masked_value), axis=1)
    shifted = logits - row_peak[:, None]
    weights = jnp.where(allowed, jnp.exp(shifted), 0.0)
    row_total = jnp.sum(weights, axis=1)
    row_moment = jnp.sum(weights * jnp.where(allowed, shifted, 0.0), axis=1)
    return (row_peak, row_total, row_moment)


def local(hidden, lm_head, positions, vocab_limits, loss_mask):
    width_dev = lm_head.shape[1]
    tokens_all = positions.shape[0]
    first_column = lax.axis_index(("seq", "vocab")) * width_dev
    full_rows = lax.all_gather(hidden, "vocab", axis=1, tiled=True)
    logits = jnp.dot(
        lax.all_gather(full_rows, "seq", axis=0, tiled=True),
        lm_head,
        preferred_element_type=jnp.float32,
    )
    fresh = row_stats(logits, vocab_limits, first_column)
    stats = tuple((newer for newer in fresh))
    local_peak, local_total, local_moment = stats
    shared_peak = lax.pmax(local_peak, ("seq", "vocab"))
    ratio = jnp.exp(local_peak - shared_peak)
    scaled_total = ratio * local_total
    scaled_moment = ratio * (local_moment + local_total * (local_peak - shared_peak))
    arranged_total = jnp.zeros((tokens_all,), jnp.float32).at[positions].set(scaled_total)
    arranged_moment = jnp.zeros((tokens_all,), jnp.float32).at[positions].set(scaled_moment)
    part_total, part_moment = (
        lax.psum_scatter(arranged_total, "seq", scatter_dimension=0, tiled=True),
        lax.psum_scatter(arranged_moment, "seq", scatter_dimension=0, tiled=True),
    )
    own_total, own_moment = lax.psum((part_total, part_moment), "vocab")
    token_entropy = jnp.log(own_total) - own_moment / own_total
    mask_float = loss_mask.astype(jnp.float32)
    masked_sum, mask_count = lax.psum(
        (jnp.sum(token_entropy * mask_float), jnp.sum(mask_float)), "seq"
    )
    mean_entropy = masked_sum / jnp.maximum(mask_count, 1.0)
    return (token_entropy, mean_entropy)


def solution(mesh):
    placed = (P("seq", "vocab"), P(None, ("seq", "vocab")), P(), P(), P("seq"))
    return jax.shard_map(
        local, mesh=mesh, in_specs=placed, out_specs=(P("seq"), P()), check_vma=False
    )
```

profile of v0, /device:TPU:0, one launch (start us, length us, event | category | flops | bytes accessed | tf_op | source)
XLA Modules:
  0.0 250.2 jit_solution(5889126691616589897)
XLA Ops:
  7.2 0.0 all-gather.2.cloned.1.call-start
  7.2 11.2 %all_gather.6 = bf16[96,3584]{1,0:T(8,128)(2,1)} all-gather(bf16[96,896]{1,0:T(8,128)(2,1)} %param.5), channel_id=1, replica_groups=mesh['seq'=8,'vocab'=4] {'vocab'}, dimensions={1}, use_global_device_ids=true | all-gather | bytes 860160 | tf_op jit(solution)/shard_map/all_gather | solution.py:24
  18.4 0.0 all-gather.2.cloned.1.call-update
  18.4 1.2 dynamic-slice
  20.3 0.7 compare_select_fusion.3
  21.0 0.0 copy-start
  21.0 87.0 %all-gather.2.cloned.1.call-done = bf16[768,3584]{1,0:T(8,128)(2,1)} async-done(((bf16[96,3584]{1,0:T(8,128)(2,1)}), bf16[768,3584]{1,0:T(8,128)(2,1)}) %all-gather.2.cloned.1.call-update) | async-done | bytes 5505040 | tf_op jit(solution)/shard_map/all_gather | solution.py:26
  108.0 33.9 %fusion = (f32[768]{0:T(1024)S(1)}, f32[768,4752]{0,1:T(8,128)}) fusion(s32[768]{0:T(1024)} %param.8, s32[4752]{0:T(1024)S(1)} %iota_add_fusion, bf16[768,3584]{1,0:T(8,128)(2,1)} %all-gather.2.cloned.1.call-done, bf16[3584,4752]{0,1:T(8,128)(2,1)} %param.6), kind=kOutput, calls=%fused_computation.5 | convolution fusion | flops 26170822656 | bytes 54190656 | tf_op jit(solution)/shard_map/dot_general | solution.py:25
  141.9 0.0 copy-start.1
  141.9 38.3 %pmax.7 = f32[768]{0:T(1024)S(1)} all-reduce(f32[768]{0:T(1024)S(1)} %get-tuple-element.15), channel_id=1, replica_groups=mesh['seq'=8,'vocab'=4] {'seq','vocab'}, use_global_device_ids=true, to_apply=%region_1.2 | all-reduce | flops 768 | bytes 6144 | tf_op jit(solution)/shard_map/pmax | solution.py:33
  180.2 0.0 copy-done
  180.2 7.9 %fusion.3 = (f32[768]{0:T(1024)S(1)}, f32[768]{0:T(1024)S(1)}) fusion(f32[768,4752]{0,1:T(8,128)} %get-tuple-element.16, f32[768]{0:T(1024)S(1)} %get-tuple-element.15, s32[768]{0:T(1024)S(1)} %copy-done, s32[4752]{0:T(1024)S(1)} %iota_add_fusion), kind=kLoop, calls=%fused_computation.8 | loop fusion | flops 25545216 | bytes 14629440 | tf_op jit(solution)/shard_map/reduce_sum | solution.py:15
  188.1 3.4 %scatter_custom_fusion = f32[768]{0:T(1024)S(1)} fusion(s32[768]{0:T(1024)S(1)} %compare_select_fusion.3, f32[768]{0:T(1024)S(1)} %get-tuple-element.13, f32[]{:T(128)} %constant.11.clone.1), kind=kCustom, calls=%fused_computation.15 | custom fusion | bytes 3076 | tf_op jit(solution)/shard_map/scatter | solution.py:37
  191.5 3.4 %scatter_custom_fusion.1 = f32[768]{0:T(1024)S(1)} fusion(s32[768]{0:T(1024)S(1)} %compare_select_fusion.3, f32[768]{0:T(1024)S(1)} %get-tuple-element.14, f32[]{:T(128)} %constant.11.clone.1), kind=kCustom, calls=%fused_computation.13 | custom fusion | bytes 3076 | tf_op jit(solution)/shard_map/scatter | solution.py:38
  194.9 21.4 %all-reduce.3 = (f32[768]{0:T(1024)S(1)}, f32[768]{0:T(1024)S(1)}) all-reduce(f32[768]{0:T(1024)S(1)} %scatter_custom_fusion.1, f32[768]{0:T(1024)S(1)} %scatter_custom_fusion), channel_id=3, replica_groups=mesh['seq'=8,'vocab'=4] {'seq'}, use_global_device_ids=true, to_apply=%region_8.9.clone | all-reduce | flops 1536 | bytes 12288
  216.3 0.1 dynamic-slice.1
  216.3 0.1 dynamic-slice.3
  216.4 5.6 %all-reduce.4 = (f32[96]{0:T(128)S(1)}, f32[96]{0:T(128)S(1)}) all-reduce(f32[96]{0:T(128)S(1)} %dynamic-slice.3, f32[96]{0:T(128)S(1)} %dynamic-slice.1), channel_id=1, replica_groups=mesh['seq'=8,'vocab'=4] {'vocab'}, use_global_device_ids=true, to_apply=%region_9.10 | all-reduce | flops 192 | bytes 1536 | tf_op jit(solution)/shard_map/psum | solution.py:43
  222.1 0.0 copy-done.1
  222.1 1.2 convert_reduce_fusion
  223.3 17.8 %all-reduce.2 = (f32[]{:T(128)}, f32[]{:T(128)}) all-reduce(f32[]{:T(128)} %get-tuple-element.5, f32[]{:T(128)} %get-tuple-element.4), channel_id=1, replica_groups=mesh['seq'=8,'vocab'=4] {'seq'}, use_global_device_ids=true, to_apply=%region_11.12 | all-reduce | flops 2 | bytes 16 | tf_op jit(solution)/shard_map/psum | solution.py:46
  (2 shorter events, 0.0 us)
Async XLA Ops:
  7.2 100.8 %all-gather.2.cloned.1.call-start = ((), (), s32[]{:S(2)}) async-start(), calls=%async_computation | async-start | bytes 6193152 | tf_op jit(solution)/shard_map/all_gather | solution.py:26
  21.0 159.2 %copy-start = (s32[768]{0:T(1024)S(1)}, s32[768]{0:T(1024)}, u32[]{:S(2)}) copy-start(s32[768]{0:T(1024)} %param.8) | copy-start | bytes 9220
  141.9 80.2 %copy-start.1 = (s32[96]{0:T(128)S(1)}, s32[96]{0:T(128)}, u32[]{:S(2)}) copy-start(s32[96]{0:T(128)} %param.9) | copy-start | bytes 1156
Sparse Core Ops, SparseCore 0:
  18.5 89.4 all-gather.1
where the time goes:
time: 251 us; the launch traced here: 250 us
  blocking collectives  94.2 us (38%)
  waiting for transfers between devices  87 us (35%)
  matrix products  33.9 us (14%)
  between operations  17.1 us (7%)
  other arithmetic  9.85 us (4%)
  local copies, waits for them, and re-layouts  8.16 us (3%)
    all_gather x1, waiting for transfers between devices, local(): lax.all_gather(full_rows, 'seq', axis=0, tiled=True)  87 us
    pmax x1, blocking collectives, local(): shared_peak = lax.pmax(local_peak, ('seq', 'vocab'))  38.3 us
    dot_general x1, matrix products, local(): jnp.dot(lax.all_gather(full_rows, 'seq', axis=0, tiled=True), lm_head, pr...  33.9 us
    unnamed x1, blocking collectives  21.4 us
    psum x1, blocking collectives, local(): lax.psum((jnp.sum(token_entropy * mask_float), jnp.sum(mask_float)), 'seq')  17.8 us
    all_gather x1, blocking collectives, local(): full_rows = lax.all_gather(hidden, 'vocab', axis=1, tiled=True)  11.2 us
    reduce_sum x1, other arithmetic, row_stats(): row_total = jnp.sum(weights, axis=1)  7.94 us
    psum x1, blocking collectives, local(): own_total, own_moment = lax.psum((part_total, part_moment), 'vocab')  5.63 us
  transfers between devices with their start and end apart: 1, of which 1 were waited for; matrix products, arithmetic and copies ran while one was open for 1% of the time, Pallas kernels for 0%

commit v1 on v0

v1 whole, which is shorter than its diff:
```python
import functools
import jax
import jax.numpy as jnp
from jax import lax
from jax.experimental import pallas as pl
from jax.experimental.pallas import tpu as pltpu
from jax.sharding import PartitionSpec as P

AXES = ("seq", "vocab")
NEG = -1e30
FAR = 1 << 30
VMEM_LIMIT = 60 * 2**20


def dot_t(a, b):
    return lax.dot_general(a, b, (((1,), (1,)), ((), ())), preferred_element_type=jnp.float32)


def fold(buf, rows, limits, base, peak, total, moment):
    for at in range(0, buf.shape[1], 128):
        lanes = slice(at, at + 128)
        room = limits[:, lanes] - base - lax.broadcasted_iota(jnp.int32, (8, 128), 0)
        old = peak[:, lanes]
        top = old
        for r in range(0, rows, 8):
            top = jnp.maximum(top, jnp.where(room > r, buf[r : r + 8, lanes], NEG))
        drop = old - top
        ratio = jnp.exp(drop)
        before = total[:, lanes]
        sums = [ratio * before, jnp.zeros_like(before)]
        moments = [ratio * (moment[:, lanes] + before * drop), jnp.zeros_like(before)]
        for r in range(0, rows, 8):
            shifted = jnp.where(room > r, buf[r : r + 8, lanes], NEG) - top
            weight = jnp.exp(shifted)
            side = r // 8 % 2
            sums[side] = sums[side] + weight
            moments[side] = moments[side] + weight * shifted
        peak[:, lanes] = top
        total[:, lanes] = sums[0] + sums[1]
        moment[:, lanes] = moments[0] + moments[1]


def stats_kernel(half, steps, slots, width, pieces, info, limits, *refs):
    blocks, (w_hbm, out, lhs, w_buf, sem, buf0, buf1, peak, total, moment) = refs[: len(pieces)], refs[len(pieces) :]
    tile = 2 * half
    first = info[0]

    def copy(step):
        slot = step % slots if isinstance(step, int) else lax.rem(step, slots)
        row = step * tile if isinstance(step, int) else pl.multiple_of(step * tile, 16)
        return pltpu.make_async_copy(w_hbm.at[pl.ds(row, tile), :], w_buf.at[slot], sem.at[slot])

    for step in range(min(slots - 1, steps)):
        copy(step).start()
    at = 1
    for block, count in zip(blocks, pieces):
        rows, depth = block.shape[1:]
        for i in range(count):
            if depth == lhs.shape[1]:
                lhs[pl.ds(pl.multiple_of(info[at], 16), rows), :] = block[i]
            else:
                lhs[pl.ds(pl.multiple_of(info[at], 16), rows), pl.ds(pl.multiple_of(info[at + 1], 128), depth)] = block[i]
            at += 2
    peak[...] = jnp.full_like(peak, NEG)
    total[...] = jnp.zeros_like(total)
    moment[...] = jnp.zeros_like(moment)
    buf1[...] = jnp.zeros_like(buf1)
    run = (limits, peak, total, moment)

    def body(step, carry):
        slot = lax.rem(step, slots)
        copy(step).wait()

        @pl.when(step + slots - 1 < steps)
        def _():
            copy(step + slots - 1).start()

        base = first + step * tile
        buf0[...] = dot_t(w_buf[slot, :half, :], lhs[...])
        fold(buf1, half, limits, jnp.where(step == 0, FAR, base - half), peak, total, moment)
        buf1[...] = dot_t(w_buf[slot, half:, :], lhs[...])
        fold(buf0, half, limits, base, peak, total, moment)
        return carry

    lax.fori_loop(0, steps, body, 0)
    fold(buf1, half, limits, first + steps * tile - half, peak, total, moment)
    top = jnp.max(peak[...], axis=0, keepdims=True)
    drop = peak[...] - top
    ratio = jnp.exp(drop)
    out[0:1, :] = top
    out[1:2, :] = jnp.sum(ratio * total[...], axis=0, keepdims=True)
    out[2:3, :] = jnp.sum(ratio * (moment[...] + total[...] * drop), axis=0, keepdims=True)


def row_stats(info, limits, blocks, w_rows, tokens, half, steps):
    depth = w_rows.shape[1]
    slots = max(2, min(4, steps))
    pieces = tuple(b.shape[0] for b in blocks)
    wide = half * 2 * steps
    return pl.pallas_call(
        functools.partial(stats_kernel, half, steps, slots, wide, pieces),
        out_shape=jax.ShapeDtypeStruct((3, tokens), jnp.float32),
        in_specs=[pl.BlockSpec(memory_space=pltpu.SMEM)]
        + [pl.BlockSpec(memory_space=pltpu.VMEM)] * (1 + len(blocks))
        + [pl.BlockSpec(memory_space=pl.ANY)],
        out_specs=pl.BlockSpec(memory_space=pltpu.VMEM),
        scratch_shapes=[
            pltpu.VMEM((tokens, depth), jnp.bfloat16),
            pltpu.VMEM((slots, 2 * half, depth), jnp.bfloat16),
            pltpu.SemaphoreType.DMA((slots,)),
            pltpu.VMEM((half, tokens), jnp.float32),
            pltpu.VMEM((half, tokens), jnp.float32),
            pltpu.VMEM((8, tokens), jnp.float32),
            pltpu.VMEM((8, tokens), jnp.float32),
            pltpu.VMEM((8, tokens), jnp.float32),
        ],
        compiler_params=pltpu.CompilerParams(vmem_limit_bytes=VMEM_LIMIT),
        cost_estimate=pl.CostEstimate(
            flops=2 * tokens * depth * wide, bytes_accessed=2 * wide * depth, transcendentals=tokens * wide
        ),
        name="row_stats",
    )(info, limits, *blocks, w_rows)


def merge(parts):
    top = jnp.max(parts[:, 0], axis=0)
    drop = parts[:, 0] - top[None]
    ratio = jnp.exp(drop)
    return top, jnp.sum(ratio * parts[:, 1], axis=0), jnp.sum(ratio * (parts[:, 2] + parts[:, 1] * drop), axis=0)


def finish_kernel(own, parts, owner, place, entropy_out, mean_out):
    groups, _, tokens = parts.shape
    each = entropy_out.shape[1]
    top, total, moment = merge(parts[...])
    entropy = (jnp.log(total) - moment / total)[None]
    hot = lax.broadcasted_iota(jnp.int32, (each, tokens), 0) == place[...]
    mine = jnp.where(hot & (owner[...] == own[0]), entropy, 0.0)
    column = jnp.sum(mine, axis=1, keepdims=True)
    square = lax.broadcasted_iota(jnp.int32, (each, each), 0) == lax.broadcasted_iota(jnp.int32, (each, each), 1)
    entropy_out[...] = jnp.sum(jnp.where(square, column, 0.0), axis=0, keepdims=True)
    mask = parts[:, 3, :each]
    at_place = jnp.dot(mask.astype(jnp.bfloat16), hot.astype(jnp.bfloat16), preferred_element_type=jnp.float32)
    group = lax.broadcasted_iota(jnp.int32, (groups, tokens), 0)
    by_row = jnp.sum(jnp.where(group == owner[...], at_place, 0.0), axis=0, keepdims=True)
    masked = jnp.sum(entropy * by_row, axis=1, keepdims=True)
    count = jnp.sum(jnp.sum(mask, axis=1, keepdims=True), axis=0, keepdims=True)
    mean_out[...] = masked / jnp.maximum(count, 1.0)


def finish(own, parts, owner, place, each):
    return pl.pallas_call(
        finish_kernel,
        out_shape=(jax.ShapeDtypeStruct((1, each), jnp.float32), jax.ShapeDtypeStruct((1, 1), jnp.float32)),
        in_specs=[pl.BlockSpec(memory_space=pltpu.SMEM)] + [pl.BlockSpec(memory_space=pltpu.VMEM)] * 3,
        out_specs=(pl.BlockSpec(memory_space=pltpu.VMEM), pl.BlockSpec(memory_space=pltpu.VMEM)),
        name="finish",
    )(own, parts, owner, place)


def swap_table(seq, vocab, moves):
    pairs = []
    for s in range(seq):
        for v in range(vocab):
            ds, dv = moves[v % 2]
            pairs.append((s * vocab + v, (s ^ ds) * vocab + (v ^ dv)))
    return pairs


def gather_plan(seq, vocab):
    plane = vocab.bit_length() - 2
    seq_bits = seq.bit_length() - 1
    stages = [((1 << b, 0), (1 << b, 0)) for b in range(plane, seq_bits)]
    for b in range(plane):
        across, along = (0, 2 << b), (1 << b, 0)
        stages += [(across, along), (along, across)]
    return stages + [((0, 1), (0, 1))]


def gather_blocks(seq, vocab, my_seq, my_vocab, hidden):
    rows, depth = hidden.shape
    stack = hidden[None]
    places = [[(0, 0)], [(0, 0)]]
    stages = gather_plan(seq, vocab)
    for n, moves in enumerate(stages):
        held = stack
        came = lax.ppermute(held, AXES, swap_table(seq, vocab, moves))
        if n < len(stages) - 1:
            stack = jnp.concatenate([held, came], axis=0)
            places = [p + [(s ^ m[0], v ^ m[1]) for s, v in p] for p, m in zip(places, moves)]
    there = [[(s, v ^ 1) for s, v in places[1]], [(s, v ^ 1) for s, v in places[0]]]
    table = jnp.array([places[c] + there[c] for c in range(2)], jnp.int32)[my_vocab % 2]
    return [held, came], (table[:, 0] ^ my_seq) * rows, (table[:, 1] ^ my_vocab) * depth


def local(seq, vocab, hidden, lm_head, positions, vocab_limits, loss_mask):
    rows, depth = hidden.shape
    columns = lm_head.shape[1]
    tokens = positions.shape[0]
    each = loss_mask.shape[0]
    my_seq, my_vocab = lax.axis_index("seq"), lax.axis_index("vocab")
    first = (my_seq * vocab + my_vocab) * columns

    if depth % 128:
        whole = lax.all_gather(lax.all_gather(hidden, "vocab", axis=1, tiled=True), "seq", axis=0, tiled=True)
        blocks = [whole[None]]
        row_at = col_at = jnp.zeros((1,), jnp.int32)
    else:
        blocks, row_at, col_at = gather_blocks(seq, vocab, my_seq, my_vocab, hidden)
    info = jnp.concatenate([first[None], jnp.stack([row_at, col_at], axis=1).reshape(-1)]).astype(jnp.int32)

    steps = max(1, round(columns / 528))
    half = -(-columns // (steps * 16)) * 8
    w_rows = lm_head.T
    spare = 2 * half * steps - columns
    limits = jnp.minimum(vocab_limits, first + columns)
    if spare:
        w_rows = jnp.pad(w_rows, ((0, spare), (0, 0)))
    limits = jnp.broadcast_to(limits[None], (8, tokens))
    stats = row_stats(info, limits, blocks, w_rows, tokens, half, steps)

    top, total, moment = merge(lax.all_gather(stats, "vocab"))
    mask = jnp.pad(loss_mask.astype(jnp.float32), (0, tokens - each))
    sent = jnp.stack([top, total, moment, mask])
    parts = lax.all_to_all(jnp.broadcast_to(sent[None], (seq, 4, tokens)), "seq", 0, 0, tiled=True)
    entropy, mean = finish(my_seq[None].astype(jnp.int32), parts, (positions // each)[None], (positions % each)[None], each)
    return entropy.reshape(each), mean.reshape(())


def solution(mesh):
    placed = (P("seq", "vocab"), P(None, AXES), P(), P(), P("seq"))
    body = functools.partial(local, mesh.shape["seq"], mesh.shape["vocab"])
    return jax.shard_map(body, mesh=mesh, in_specs=placed, out_specs=(P("seq"), P()), check_vma=False)
```

time: 251 us -> 122 us (0.49)
  blocking collectives: 94.2 us -> 5.43 us
  Pallas kernels: 0 us -> 37.7 us
  matrix products: 33.9 us -> 0 us
  waiting for transfers between devices: 87 us -> 55.5 us
  between operations: 17.1 us -> 0.88 us
  starting transfers between devices: 0.04 us -> 14.5 us
  other arithmetic: 9.85 us -> 4.08 us
  local copies, waits for them, and re-layouts: 8.16 us -> 3.72 us
    all_gather x1 -> x0, waiting for transfers between devices: 87 us -> none  [local(): lax.all_gather(full_rows, 'seq', axis=0, tiled=True)]
    ppermute x0 -> x5, waiting for transfers between devices: none -> 49.6 us  [gather_blocks(): came = lax.ppermute(held, AXES, swap_table(seq, vocab, moves))]
    pmax x1 -> x0, blocking collectives: 38.3 us -> none  [local(): shared_peak = lax.pmax(local_peak, ('seq', 'vocab'))]
    pallas_call x0 -> x2, Pallas kernels: none -> 37.7 us  [the longest x1 36 us: row_stats(): pl.pallas_call(functools.partial(stats_kernel, half, steps, slots, wide,...]
    dot_general x1 -> x0, matrix products: 33.9 us -> none  [local(): jnp.dot(lax.all_gather(full_rows, 'seq', axis=0, tiled=True), lm_head, pr...]
    psum x2 -> x0, blocking collectives: 23.4 us -> none  [the longest x1 17.8 us: local(): lax.psum((jnp.sum(token_entropy * mask_float), jnp.sum(mask_float)), 'seq')]
    unnamed x1 -> x0, blocking collectives: 21.4 us -> none
    reduce_sum x2 -> x1, other arithmetic: 9.14 us -> 0.03 us  [merge(): jnp.sum(ratio * parts[:, 1], axis=0)]
  transfers between devices with their start and end apart: 1 -> 6, of which waited for: 1 -> 6; matrix products, arithmetic and copies ran while one was open for 1% -> 2% of each run, Pallas kernels for 0% -> 0%
where the time goes in v1:
time: 122 us
  waiting for transfers between devices  55.5 us (45%)
  Pallas kernels  37.7 us (31%)
  starting transfers between devices  14.5 us (12%)
  blocking collectives  5.43 us (4%)
  other arithmetic  4.08 us (3%)
  local copies, waits for them, and re-layouts  3.72 us (3%)
    ppermute x5, waiting for transfers between devices, gather_blocks(): came = lax.ppermute(held, AXES, swap_table(seq, vocab, moves))  49.6 us
    pallas_call x1, Pallas kernels, row_stats(): pl.pallas_call(functools.partial(stats_kernel, half, steps, slots, wide,...  36 us
    ppermute x5, starting transfers between devices, gather_blocks(): came = lax.ppermute(held, AXES, swap_table(seq, vocab, moves))  8.91 us
    all_to_all x1, waiting for transfers between devices, local(): lax.all_to_all(jnp.broadcast_to(sent[None], (seq, 4, tokens)), 'seq', 0,...  5.92 us
    all_to_all x1, starting transfers between devices, local(): lax.all_to_all(jnp.broadcast_to(sent[None], (seq, 4, tokens)), 'seq', 0,...  5.6 us
    all_gather x1, blocking collectives, local(): top, total, moment = merge(lax.all_gather(stats, 'vocab'))  5.43 us
    concatenate x3, other arithmetic, gather_blocks(): stack = jnp.concatenate([held, came], axis=0)  3.05 us
  transfers between devices with their start and end apart: 6, of which 6 were waited for; matrix products, arithmetic and copies ran while one was open for 2% of the time, Pallas kernels for 0%

profile of v1, /device:TPU:0, one launch (start us, length us, event | category | flops | bytes accessed | tf_op | source)
XLA Modules:
  0.0 121.8 jit_solution(203795360304212253)
XLA Ops:
  0.6 0.0 copy-start
  0.6 3.1 %collective-permute-start = (bf16[1,96,896]{2,1,0:T(8,128)(2,1)}, bf16[1,96,896]{2,1,0:T(8,128)(2,1)S(1)}, u32[]{:S(2)}, u32[]{:S(2)}) collective-permute-start(bf16[1,96,896]{2,1,0:T(8,128)(2,1)} %bitcast.33), channel_id=1, source_target_pairs={{0,8},{1,9},{2,10},{3,11},{4,12},{5,13},{6,14},{7,15},{8,0},{9,1},... | collective-permute-start | bytes 516104 | tf_op jit(solution)/shard_map/ppermute | solution.py:187
  3.8 4.6 %collective-permute-done = bf16[1,96,896]{2,1,0:T(8,128)(2,1)S(1)} collective-permute-done((bf16[1,96,896]{2,1,0:T(8,128)(2,1)}, bf16[1,96,896]{2,1,0:T(8,128)(2,1)S(1)}, u32[]{:S(2)}, u32[]{:S(2)}) %collective-permute-start) | collective-permute-done | bytes 172064 | tf_op jit(solution)/shard_map/ppermute | solution.py:187
  8.3 1.0 pad_maximum_fusion.2
  9.3 2.8 %collective-permute-start.1 = (bf16[2,96,896]{2,1,0:T(8,128)(2,1)S(1)}, bf16[2,96,896]{2,1,0:T(8,128)(2,1)S(1)}, u32[]{:S(2)}, u32[]{:S(2)}) collective-permute-start(bf16[2,96,896]{2,1,0:T(8,128)(2,1)S(1)} %pad_maximum_fusion.2), channel_id=1, source_target_pairs={{0,16},{1,17},{2,18},{3,19},{4,20},{5,21},{6,22},{7,23},{8,24},{9,... | collective-permute-start | bytes 1032200 | tf_op jit(solution)/shard_map/ppermute | solution.py:187
  12.1 14.7 %collective-permute-done.1 = bf16[2,96,896]{2,1,0:T(8,128)(2,1)S(1)} collective-permute-done((bf16[2,96,896]{2,1,0:T(8,128)(2,1)S(1)}, bf16[2,96,896]{2,1,0:T(8,128)(2,1)S(1)}, u32[]{:S(2)}, u32[]{:S(2)}) %collective-permute-start.1) | collective-permute-done | bytes 344096 | tf_op jit(solution)/shard_map/ppermute | solution.py:187
  26.9 1.0 pad_maximum_fusion.1
  27.9 1.4 %collective-permute-start.2 = (bf16[4,96,896]{2,1,0:T(8,128)(2,1)S(1)}, bf16[4,96,896]{2,1,0:T(8,128)(2,1)S(1)}, u32[]{:S(2)}, u32[]{:S(2)}) collective-permute-start(bf16[4,96,896]{2,1,0:T(8,128)(2,1)S(1)} %pad_maximum_fusion.1), channel_id=1, source_target_pairs={{0,2},{1,5},{2,0},{3,7},{4,6},{5,1},{6,4},{7,3},{8,10},{9,13},{10,... | collective-permute-start | bytes 2064392 | tf_op jit(solution)/shard_map/ppermute | solution.py:187
  29.3 9.6 %collective-permute-done.2 = bf16[4,96,896]{2,1,0:T(8,128)(2,1)S(1)} collective-permute-done((bf16[4,96,896]{2,1,0:T(8,128)(2,1)S(1)}, bf16[4,96,896]{2,1,0:T(8,128)(2,1)S(1)}, u32[]{:S(2)}, u32[]{:S(2)}) %collective-permute-start.2) | collective-permute-done | bytes 688160 | tf_op jit(solution)/shard_map/ppermute | solution.py:187
  38.9 1.1 pad_maximum_fusion
  40.0 0.0 copy-start.6
  40.0 0.0 copy-start.5
  40.0 0.0 copy-start.4
  40.0 1.5 %collective-permute-start.3 = (bf16[8,96,896]{2,1,0:T(8,128)(2,1)S(1)}, bf16[8,96,896]{2,1,0:T(8,128)(2,1)S(1)}, u32[]{:S(2)}, u32[]{:S(2)}) collective-permute-start(bf16[8,96,896]{2,1,0:T(8,128)(2,1)S(1)} %pad_maximum_fusion), channel_id=1, source_target_pairs={{0,4},{1,3},{2,6},{3,1},{4,0},{5,7},{6,2},{7,5},{8,12},{9,11},{10,... | collective-permute-start | bytes 4128776 | tf_op jit(solution)/shard_map/ppermute | solution.py:187
  41.5 0.0 copy-done
  41.6 0.1 constant_dynamic-update-slice_fusion.1
  41.7 16.7 %collective-permute-done.3 = bf16[8,96,896]{2,1,0:T(8,128)(2,1)S(1)} collective-permute-done((bf16[8,96,896]{2,1,0:T(8,128)(2,1)S(1)}, bf16[8,96,896]{2,1,0:T(8,128)(2,1)S(1)}, u32[]{:S(2)}, u32[]{:S(2)}) %collective-permute-start.3) | collective-permute-done | bytes 1376288 | tf_op jit(solution)/shard_map/ppermute | solution.py:187
  58.4 0.2 constant_dynamic-update-slice_fusion.refs_0_
  58.6 0.0 copy-start.2
  58.6 0.1 collective-permute-start.4
  58.7 0.0 copy-done.6
  58.8 0.0 copy-done.5
  58.8 0.1 copy.14
  58.9 0.1 reshape.16
  59.0 0.9 pad_add_fusion.1.info
  59.9 0.0 copy-done.4
  59.9 4.0 %collective-permute-done.4.refs_1_ = bf16[16,96,896]{2,1,0:T(8,128)(2,1)} collective-permute-done((bf16[16,96,896]{2,1,0:T(8,128)(2,1)S(1)}, bf16[16,96,896]{2,1,0:T(8,128)(2,1)}, u32[]{:S(2)}, u32[]{:S(2)}) %collective-permute-start.4) | collective-permute-done | bytes 2752544 | tf_op jit(solution)/shard_map/ppermute | solution.py:187
  63.9 0.6 broadcast_in_dim.30.limits
  64.5 0.0 copy-done.2
  64.5 0.0 copy-start.3
  64.5 36.0 %row_stats.1 = f32[3,768]{1,0:T(4,128)} custom-call(s32[65]{0:T(128)} %pad_add_fusion.1.info, s32[8,768]{1,0:T(8,128)} %broadcast_in_dim.30.limits, bf16[16,96,896]{2,1,0:T(8,128)(2,1)} %copy-done.2, bf16[16,96,896]{2,1,0:T(8,128)(2,1)} %collective-permute-done.4.refs_1_, bf16[4752,3584]{1,0:T(8,128)(2,1)} %bitcast.38), custom_call_target="tpu_custom_call" | custom-call | flops 26159874048 | bytes 34062336 | tf_op jit(solution)/shard_map/row_stats/pallas_call | solution.py:100
  100.6 5.4 %all-gather.1 = f32[4,3,768]{2,1,0:T(4,128)S(1)} all-gather(f32[1,3,768]{2,1,0:T(4,128)} %bitcast.37), channel_id=2, replica_groups=mesh['seq'=8,'vocab'=4] {'vocab'}, dimensions={0}, use_global_device_ids=true | all-gather | bytes 46080 | tf_op jit(solution)/shard_map/all_gather | solution.py:222
  106.1 0.7 broadcast_in_dim.32
  106.8 5.6 %all-to-all-start = ((f32[8,4,768]{2,1,0:T(4,128)}), f32[8,4,768]{2,1,0:T(4,128)S(1)}, u32[]{:S(2)}, u32[]{:S(2)}) async-start(f32[8,4,768]{2,1,0:T(4,128)} %broadcast_in_dim.32), calls=%async_computation | async-start | bytes 196608 | tf_op jit(solution)/shard_map/all_to_all | solution.py:225
  112.4 0.0 copy-done.3
  112.4 0.6 broadcast_in_dim.33.owner
  113.0 0.6 broadcast_in_dim.34.place
  113.6 5.9 %all-to-all-done.parts = f32[8,4,768]{2,1,0:T(4,128)S(1)} async-done(((f32[8,4,768]{2,1,0:T(4,128)}), f32[8,4,768]{2,1,0:T(4,128)S(1)}, u32[]{:S(2)}, u32[]{:S(2)}) %all-to-all-start) | async-done | bytes 98336 | tf_op jit(solution)/shard_map/all_to_all | solution.py:225
  119.5 0.0 copy-start.1
  119.5 0.6 copy-done.1
  120.2 1.7 %finish.1 = (f32[1,96]{1,0:T(1,128)}, f32[1,1]{1,0:T(1,128)}) custom-call(s32[1]{0:T(128)} %bitcast.own, f32[8,4,768]{2,1,0:T(4,128)} %copy-done.1, s32[1,768]{1,0:T(1,128)} %broadcast_in_dim.33.owner, s32[1,768]{1,0:T(1,128)} %broadcast_in_dim.34.place), custom_call_target="tpu_custom_call" | custom-call | tf_op jit(solution)/shard_map/finish/pallas_call | solution.py:152
  (17 shorter events, 0.2 us)
Async XLA Ops:
  0.6 40.8 %copy-start = (bf16[96,896]{1,0:T(8,128)(2,1)S(1)}, bf16[96,896]{1,0:T(8,128)(2,1)}, u32[]{:S(2)}) copy-start(bf16[96,896]{1,0:T(8,128)(2,1)} %param.6) | copy-start | bytes 516100
  0.6 7.7 %collective-permute-start = (bf16[1,96,896]{2,1,0:T(8,128)(2,1)}, bf16[1,96,896]{2,1,0:T(8,128)(2,1)S(1)}, u32[]{:S(2)}, u32[]{:S(2)}) collective-permute-start(bf16[1,96,896]{2,1,0:T(8,128)(2,1)} %bitcast.33), channel_id=1, source_target_pairs={{0,8},{1,9},{2,10},{3,11},{4,12},{5,13},{6,14},{7,15},{8,0},{9,1},... | collective-permute-start | bytes 516104 | tf_op jit(solution)/shard_map/ppermute | solution.py:187
  9.3 17.6 %collective-permute-start.1 = (bf16[2,96,896]{2,1,0:T(8,128)(2,1)S(1)}, bf16[2,96,896]{2,1,0:T(8,128)(2,1)S(1)}, u32[]{:S(2)}, u32[]{:S(2)}) collective-permute-start(bf16[2,96,896]{2,1,0:T(8,128)(2,1)S(1)} %pad_maximum_fusion.2), channel_id=1, source_target_pairs={{0,16},{1,17},{2,18},{3,19},{4,20},{5,21},{6,22},{7,23},{8,24},{9,... | collective-permute-start | bytes 1032200 | tf_op jit(solution)/shard_map/ppermute | solution.py:187
  27.9 11.0 %collective-permute-start.2 = (bf16[4,96,896]{2,1,0:T(8,128)(2,1)S(1)}, bf16[4,96,896]{2,1,0:T(8,128)(2,1)S(1)}, u32[]{:S(2)}, u32[]{:S(2)}) collective-permute-start(bf16[4,96,896]{2,1,0:T(8,128)(2,1)S(1)} %pad_maximum_fusion.1), channel_id=1, source_target_pairs={{0,2},{1,5},{2,0},{3,7},{4,6},{5,1},{6,4},{7,3},{8,10},{9,13},{10,... | collective-permute-start | bytes 2064392 | tf_op jit(solution)/shard_map/ppermute | solution.py:187
  40.0 18.7 %copy-start.6 = (s32[96]{0:T(128)S(1)}, s32[96]{0:T(128)}, u32[]{:S(2)}) copy-start(s32[96]{0:T(128)} %param.10) | copy-start | bytes 1156
  40.0 18.8 %copy-start.5 = (s32[2,32,2]{1,2,0:T(2,128)S(1)}, s32[2,32,2]{1,2,0:T(2,128)}, u32[]{:S(2)}) copy-start(s32[2,32,2]{1,2,0:T(2,128)} %constant.55.clone) | copy-start | bytes 1540
  40.0 19.9 %copy-start.4 = (s32[768]{0:T(1024)S(1)}, s32[768]{0:T(1024)}, u32[]{:S(2)}) copy-start(s32[768]{0:T(1024)} %param.9) | copy-start | bytes 9220
  40.0 18.4 %collective-permute-start.3 = (bf16[8,96,896]{2,1,0:T(8,128)(2,1)S(1)}, bf16[8,96,896]{2,1,0:T(8,128)(2,1)S(1)}, u32[]{:S(2)}, u32[]{:S(2)}) collective-permute-start(bf16[8,96,896]{2,1,0:T(8,128)(2,1)S(1)} %pad_maximum_fusion), channel_id=1, source_target_pairs={{0,4},{1,3},{2,6},{3,1},{4,0},{5,7},{6,2},{7,5},{8,12},{9,11},{10,... | collective-permute-start | bytes 4128776 | tf_op jit(solution)/shard_map/ppermute | solution.py:187
  58.6 5.9 %copy-start.2 = (bf16[16,96,896]{2,1,0:T(8,128)(2,1)}, bf16[16,96,896]{2,1,0:T(8,128)(2,1)S(1)}, u32[]{:S(2)}) copy-start(bf16[16,96,896]{2,1,0:T(8,128)(2,1)S(1)} %constant_dynamic-update-slice_fusion.refs_0_) | copy-start | bytes 8257540
  58.6 5.3 %collective-permute-start.4 = (bf16[16,96,896]{2,1,0:T(8,128)(2,1)S(1)}, bf16[16,96,896]{2,1,0:T(8,128)(2,1)}, u32[]{:S(2)}, u32[]{:S(2)}) collective-permute-start(bf16[16,96,896]{2,1,0:T(8,128)(2,1)S(1)} %constant_dynamic-update-slice_fusion.refs_0_), channel_id=1, source_target_pairs={{0,1},{1,0},{2,3},{3,2},{4,5},{5,4},{6,7},{7,6},{8,9},{9,8},{10,11... | collective-permute-start | bytes 8257544 | tf_op jit(solution)/shard_map/ppermute | solution.py:187
  64.5 47.9 %copy-start.3 = (s32[768]{0:T(1024)S(1)}, s32[768]{0:T(1024)}, u32[]{:S(2)}) copy-start(s32[768]{0:T(1024)} %param.8) | copy-start | bytes 9220
  106.8 12.7 %all-to-all-start = ((f32[8,4,768]{2,1,0:T(4,128)}), f32[8,4,768]{2,1,0:T(4,128)S(1)}, u32[]{:S(2)}, u32[]{:S(2)}) async-start(f32[8,4,768]{2,1,0:T(4,128)} %broadcast_in_dim.32), calls=%async_computation | async-start | bytes 196608 | tf_op jit(solution)/shard_map/all_to_all | solution.py:225
  119.5 0.6 copy-start.1

commit v2 on v1

--- a/solution.py
+++ b/solution.py
@@ -1,4 +1,6 @@
 import functools
+import math
+
 import jax
 import jax.numpy as jnp
 from jax import lax
@@ -6,10 +8,10 @@
 from jax.experimental.pallas import tpu as pltpu
 from jax.sharding import PartitionSpec as P
 
+
 AXES = ("seq", "vocab")
 NEG = -1e30
 FAR = 1 << 30
-VMEM_LIMIT = 60 * 2**20
 
 
 def dot_t(a, b):
@@ -40,8 +42,8 @@
         moment[:, lanes] = moments[0] + moments[1]
 
 
-def stats_kernel(half, steps, slots, width, pieces, info, limits, *refs):
-    blocks, (w_hbm, out, lhs, w_buf, sem, buf0, buf1, peak, total, moment) = refs[: len(pieces)], refs[len(pieces) :]
+def stats_kernel(half, steps, slots, moves, info, limits, w_hbm, *refs):
+    arrays, (out, lhs, w_buf, sem, buf0, buf1, peak, total, moment) = refs[:-9], refs[-9:]
     tile = 2 * half
     first = info[0]
 
@@ -53,19 +55,19 @@
     for step in range(min(slots - 1, steps)):
         copy(step).start()
     at = 1
-    for block, count in zip(blocks, pieces):
-        rows, depth = block.shape[1:]
-        for i in range(count):
-            if depth == lhs.shape[1]:
-                lhs[pl.ds(pl.multiple_of(info[at], 16), rows), :] = block[i]
-            else:
-                lhs[pl.ds(pl.multiple_of(info[at], 16), rows), pl.ds(pl.multiple_of(info[at + 1], 128), depth)] = block[i]
-            at += 2
+    for array, start, rows, row in moves:
+        depth = arrays[array].shape[2]
+        to_row = pl.multiple_of(info[at + 1], 16) if row is None else row
+        block = arrays[array][info[at], start : start + rows, :]
+        if depth == lhs.shape[1]:
+            lhs[pl.ds(to_row, rows), :] = block
+        else:
+            lhs[pl.ds(to_row, rows), pl.ds(pl.multiple_of(info[at + 2], 128), depth)] = block
+        at += 3
     peak[...] = jnp.full_like(peak, NEG)
     total[...] = jnp.zeros_like(total)
     moment[...] = jnp.zeros_like(moment)
     buf1[...] = jnp.zeros_like(buf1)
-    run = (limits, peak, total, moment)
 
     def body(step, carry):
         slot = lax.rem(step, slots)
@@ -92,17 +94,24 @@
     out[2:3, :] = jnp.sum(ratio * (moment[...] + total[...] * drop), axis=0, keepdims=True)
 
 
-def row_stats(info, limits, blocks, w_rows, tokens, half, steps):
+def row_numbers(first, moves):
+    numbers = [first]
+    for _, index, _, _, row, column in moves:
+        numbers += [index, row, column]
+    return jnp.stack([jnp.asarray(n, jnp.int32) for n in numbers])
+
+
+def row_stats(info, limits, arrays, moves, w_rows, half, steps, limit):
     depth = w_rows.shape[1]
+    tokens = limits.shape[1]
+    fixed = tuple((m[0], m[2], m[3], m[4] if isinstance(m[4], int) else None) for m in moves)
+    wide = half * 2 * steps
     slots = max(2, min(4, steps))
-    pieces = tuple(b.shape[0] for b in blocks)
-    wide = half * 2 * steps
     return pl.pallas_call(
-        functools.partial(stats_kernel, half, steps, slots, wide, pieces),
+        functools.partial(stats_kernel, half, steps, slots, fixed),
         out_shape=jax.ShapeDtypeStruct((3, tokens), jnp.float32),
-        in_specs=[pl.BlockSpec(memory_space=pltpu.SMEM)]
-        + [pl.BlockSpec(memory_space=pltpu.VMEM)] * (1 + len(blocks))
-        + [pl.BlockSpec(memory_space=pl.ANY)],
+        in_specs=[pl.BlockSpec(memory_space=pltpu.SMEM), pl.BlockSpec(memory_space=pltpu.VMEM), pl.BlockSpec(memory_space=pl.ANY)]
+        + [pl.BlockSpec(memory_space=pltpu.VMEM)] * len(arrays),
         out_specs=pl.BlockSpec(memory_space=pltpu.VMEM),
         scratch_shapes=[
             pltpu.VMEM((tokens, depth), jnp.bfloat16),
@@ -114,12 +123,12 @@
             pltpu.VMEM((8, tokens), jnp.float32),
             pltpu.VMEM((8, tokens), jnp.float32),
         ],
-        compiler_params=pltpu.CompilerParams(vmem_limit_bytes=VMEM_LIMIT),
+        compiler_params=pltpu.CompilerParams(vmem_limit_bytes=limit),
         cost_estimate=pl.CostEstimate(
             flops=2 * tokens * depth * wide, bytes_accessed=2 * wide * depth, transcendentals=tokens * wide
         ),
         name="row_stats",
-    )(info, limits, *blocks, w_rows)
+    )(info, limits, w_rows, *arrays)
 
 
 def merge(parts):
@@ -132,7 +141,7 @@
 def finish_kernel(own, parts, owner, place, entropy_out, mean_out):
     groups, _, tokens = parts.shape
     each = entropy_out.shape[1]
-    top, total, moment = merge(parts[...])
+    _, total, moment = merge(parts[...])
     entropy = (jnp.log(total) - moment / total)[None]
     hot = lax.broadcasted_iota(jnp.int32, (each, tokens), 0) == place[...]
     mine = jnp.where(hot & (owner[...] == own[0]), entropy, 0.0)
@@ -158,70 +167,132 @@
     )(own, parts, owner, place)
 
 
-def swap_table(seq, vocab, moves):
+def permute(seq, vocab, array, moves):
     pairs = []
     for s in range(seq):
         for v in range(vocab):
             ds, dv = moves[v % 2]
             pairs.append((s * vocab + v, (s ^ ds) * vocab + (v ^ dv)))
-    return pairs
-
-
-def gather_plan(seq, vocab):
-    plane = vocab.bit_length() - 2
-    seq_bits = seq.bit_length() - 1
-    stages = [((1 << b, 0), (1 << b, 0)) for b in range(plane, seq_bits)]
-    for b in range(plane):
-        across, along = (0, 2 << b), (1 << b, 0)
-        stages += [(across, along), (along, across)]
-    return stages + [((0, 1), (0, 1))]
-
-
-def gather_blocks(seq, vocab, my_seq, my_vocab, hidden):
+    return lax.ppermute(array, AXES, pairs)
+
+
+def both(ds, dv):
+    return ((ds, dv), (ds, dv))
+
+
+def xor_blocks(array, groups, me):
+    shape = array.shape
+    bit = 1
+    while bit < groups:
+        halves = array.reshape(shape[:-1] + (groups // (2 * bit), 2, bit * (shape[-1] // groups)))
+        array = jnp.where(me & bit, halves[..., ::-1, :].reshape(shape), array)
+        bit *= 2
+    return array
+
+
+def overlapped(seq, vocab, my_seq, my_vocab, first, hidden, limits, w_rows, half, steps):
     rows, depth = hidden.shape
-    stack = hidden[None]
-    places = [[(0, 0)], [(0, 0)]]
-    stages = gather_plan(seq, vocab)
-    for n, moves in enumerate(stages):
-        held = stack
-        came = lax.ppermute(held, AXES, swap_table(seq, vocab, moves))
-        if n < len(stages) - 1:
-            stack = jnp.concatenate([held, came], axis=0)
-            places = [p + [(s ^ m[0], v ^ m[1]) for s, v in p] for p, m in zip(places, moves)]
-    there = [[(s, v ^ 1) for s, v in places[1]], [(s, v ^ 1) for s, v in places[0]]]
-    table = jnp.array([places[c] + there[c] for c in range(2)], jnp.int32)[my_vocab % 2]
-    return [held, came], (table[:, 0] ^ my_seq) * rows, (table[:, 1] ^ my_vocab) * depth
+    tokens = rows * seq
+    core = my_vocab % 2
+    swap = functools.partial(permute, seq, vocab)
+    x_or_y, y_or_x, cores = ((0, 2), (1, 0)), ((1, 0), (0, 2)), both(0, 1)
+    own = hidden[None]
+    limits = jnp.broadcast_to(xor_blocks(limits, seq, my_seq)[None], (8, tokens))
+    ready = 4 * rows // 256 * 256
+    early, late = [], []
+    for side in range(2):
+        c = core ^ side
+        for j in range(2):
+            for i in range(2):
+                index = jnp.where(c == 0, 2 * j + i, j + 2 * i)
+                column = ((my_vocab ^ (2 * i)) // 2 * 2 + c) * depth
+                early.append((side, index, 0, rows, j * rows, column))
+                row = (2 + j) * rows
+                cut = min(max(ready - row, 0), rows)
+                if cut:
+                    early.append((2 + side, index, 0, cut, row, column))
+                if cut < rows:
+                    late.append((side, index, cut, rows - cut, row + cut - ready, column))
+        for part in range(4):
+            j, i = ((0, 0), (0, 1), (1, 0), (1, 1))[part]
+            for k in range(seq // 2 - 2):
+                column = ((my_vocab ^ (2 * i)) // 2 * 2 + c) * depth
+                late.append((2 + 4 * side + part, k, 0, rows, (2 * (k + 2) + j) * rows - ready, column))
+    early_info, late_info = row_numbers(first, early), row_numbers(first, late)
+    early_limits, late_limits = limits[:, :ready], limits[:, ready:]
+
+    near = swap(own, both(2, 0))
+    own_x = swap(own, x_or_y)
+    own_w = swap(own, y_or_x)
+    far = []
+    for k in range(2, seq // 2):
+        far.append(swap(own, both(2 * k, 0)))
+    tables = (early_info, late_info, early_limits, late_limits)
+    own_x, (early_info, late_info, early_limits, late_limits) = lax.optimization_barrier((own_x, tables))
+    own_d = swap(own_x, y_or_x)
+    near_x = swap(near, x_or_y)
+    near_w = swap(near, y_or_x)
+    near_d = swap(near_x, y_or_x)
+    mine = jnp.concatenate([own, own_x, own_w, own_d], axis=0)
+    theirs = swap(mine, cores)
+    near_mine = jnp.concatenate([near, near_x, near_w, near_d], axis=0)
+    near_theirs = swap(near_mine, cores)
+    far_parts = [jnp.concatenate(far, axis=0)]
+    for move in (both(0, 2), both(1, 0), both(1, 2)):
+        far_parts.append(swap(far_parts[0], move))
+    far_theirs = []
+    for part in far_parts:
+        far_theirs.append(swap(part, cores))
+
+    done = row_stats(
+        early_info, early_limits, [mine, theirs, near_mine, near_theirs], early, w_rows, half, steps, 30 * 2**20
+    )
+    arrays = [near_mine, near_theirs, *far_parts, *far_theirs]
+    rest = row_stats(late_info, late_limits, arrays, late, w_rows, half, steps, 30 * 2**20)
+    return jnp.concatenate([done, rest], axis=1)
 
 
 def local(seq, vocab, hidden, lm_head, positions, vocab_limits, loss_mask):
-    rows, depth = hidden.shape
+    _, depth = hidden.shape
     columns = lm_head.shape[1]
     tokens = positions.shape[0]
     each = loss_mask.shape[0]
     my_seq, my_vocab = lax.axis_index("seq"), lax.axis_index("vocab")
     first = (my_seq * vocab + my_vocab) * columns
-
-    if depth % 128:
-        whole = lax.all_gather(lax.all_gather(hidden, "vocab", axis=1, tiled=True), "seq", axis=0, tiled=True)
-        blocks = [whole[None]]
-        row_at = col_at = jnp.zeros((1,), jnp.int32)
-    else:
-        blocks, row_at, col_at = gather_blocks(seq, vocab, my_seq, my_vocab, hidden)
-    info = jnp.concatenate([first[None], jnp.stack([row_at, col_at], axis=1).reshape(-1)]).astype(jnp.int32)
-
     steps = max(1, round(columns / 528))
     half = -(-columns // (steps * 16)) * 8
     w_rows = lm_head.T
     spare = 2 * half * steps - columns
-    limits = jnp.minimum(vocab_limits, first + columns)
     if spare:
         w_rows = jnp.pad(w_rows, ((0, spare), (0, 0)))
-    limits = jnp.broadcast_to(limits[None], (8, tokens))
-    stats = row_stats(info, limits, blocks, w_rows, tokens, half, steps)
+    limits = jnp.minimum(vocab_limits, first + columns)
+    if depth % 128 == 0 and vocab // 2 == 2 and seq >= 8:
+        stats = overlapped(seq, vocab, my_seq, my_vocab, first, hidden, limits, w_rows, half, steps)
+    else:
+        whole = lax.all_gather(lax.all_gather(hidden, "vocab", axis=1, tiled=True), "seq", axis=0, tiled=True)
+        part = math.gcd(tokens, 512)
+        stats = jnp.concatenate(
+            [
+                row_stats(
+                    row_numbers(first, [(0, 0, 0, part, 0, 0)]),
+                    jnp.broadcast_to(limits[None, at : at + part], (8, part)),
+                    [whole[None, at : at + part]],
+                    [(0, 0, 0, part, 0, 0)],
+                    w_rows,
+                    half,
+                    steps,
+                    40 * 2**20,
+                )
+                for at in range(0, tokens, part)
+            ],
+            axis=1,
+        )
+        stats = xor_blocks(stats, seq, my_seq)
 
     top, total, moment = merge(lax.all_gather(stats, "vocab"))
     mask = jnp.pad(loss_mask.astype(jnp.float32), (0, tokens - each))
-    sent = jnp.stack([top, total, moment, mask])
+    sent = xor_blocks(jnp.stack([top, total, moment]), seq, my_seq)
+    sent = jnp.concatenate([sent, mask[None]], axis=0)
     parts = lax.all_to_all(jnp.broadcast_to(sent[None], (seq, 4, tokens)), "seq", 0, 0, tiled=True)
     entropy, mean = finish(my_seq[None].astype(jnp.int32), parts, (positions // each)[None], (positions % each)[None], each)
     return entropy.reshape(each), mean.reshape(())
@@ -229,5 +300,8 @@
 
 def solution(mesh):
     placed = (P("seq", "vocab"), P(None, AXES), P(), P(), P("seq"))
-    body = functools.partial(local, mesh.shape["seq"], mesh.shape["vocab"])
+
+    def body(*args):
+        return local(mesh.shape["seq"], mesh.shape["vocab"], *args)
+
     return jax.shard_map(body, mesh=mesh, in_specs=placed, out_specs=(P("seq"), P()), check_vma=False)

time: 122 us -> 113 us (0.926)
  waiting for transfers between devices: 55.5 us -> 32 us
  starting transfers between devices: 14.5 us -> 26.1 us
  Pallas kernels: 37.7 us -> 40.2 us
    ppermute x5 -> x18, waiting for transfers between devices: 49.6 us -> 26 us  [permute(): return lax.ppermute(array, AXES, pairs)]
    ppermute x5 -> x18, starting transfers between devices: 8.91 us -> 20.6 us  [permute(): return lax.ppermute(array, AXES, pairs)]
    concatenate x4 -> x2, other arithmetic: 3.95 us -> 1.03 us  [the longest x1 1.02 us: overlapped(): mine = jnp.concatenate([own, own_x, own_w, own_d], axis=0)]
    pallas_call x1 -> x2, Pallas kernels: 36 us -> 38.5 us  [row_stats(): pl.pallas_call(functools.partial(stats_kernel, half, steps, slots, fixed)...]
  transfers between devices with their start and end apart: 6 -> 19, of which waited for: 6 -> 7; matrix products, arithmetic and copies ran while one was open for 2% -> 5% of each run, Pallas kernels for 0% -> 13%
where the time goes in v2:
time: 113 us; the launch traced here: 112 us
  Pallas kernels  40.2 us (36%)
  waiting for transfers between devices  32 us (28%)
  starting transfers between devices  26.1 us (23%)
  blocking collectives  5.22 us (5%)
  local copies, waits for them, and re-layouts  4.66 us (4%)
  other arithmetic  3.23 us (3%)
    pallas_call x2, Pallas kernels, row_stats(): pl.pallas_call(functools.partial(stats_kernel, half, steps, slots, fixed)...  38.5 us
    ppermute x18, waiting for transfers between devices, permute(): return lax.ppermute(array, AXES, pairs)  26 us
    ppermute x18, starting transfers between devices, permute(): return lax.ppermute(array, AXES, pairs)  20.6 us
    all_to_all x1, waiting for transfers between devices, local(): lax.all_to_all(jnp.broadcast_to(sent[None], (seq, 4, tokens)), 'seq', 0,...  5.93 us
    all_to_all x1, starting transfers between devices, local(): lax.all_to_all(jnp.broadcast_to(sent[None], (seq, 4, tokens)), 'seq', 0,...  5.48 us
    all_gather x1, blocking collectives, local(): top, total, moment = merge(lax.all_gather(stats, 'vocab'))  5.22 us
  transfers between devices with their start and end apart: 19, of which 7 were waited for; matrix products, arithmetic and copies ran while one was open for 5% of the time, Pallas kernels for 13%

profile of v2, /device:TPU:0, one launch (start us, length us, event | category | flops | bytes accessed | tf_op | source)
XLA Modules:
  0.0 112.3 jit_solution(4155216069054540289)
XLA Ops:
  0.6 3.0 %collective-permute-start = (bf16[1,96,896]{2,1,0:T(8,128)(2,1)}, bf16[1,96,896]{2,1,0:T(8,128)(2,1)S(1)}, u32[]{:S(2)}, u32[]{:S(2)}) collective-permute-start(bf16[1,96,896]{2,1,0:T(8,128)(2,1)} %bitcast.45), channel_id=1, source_target_pairs={{0,2},{1,5},{2,0},{3,7},{4,6},{5,1},{6,4},{7,3},{8,10},{9,13},{10,... | collective-permute-start | bytes 516104 | tf_op jit(solution)/shard_map/ppermute | solution.py:176
  3.7 1.5 %collective-permute-start.1 = (bf16[1,96,896]{2,1,0:T(8,128)(2,1)}, bf16[1,96,896]{2,1,0:T(8,128)(2,1)S(1)}, u32[]{:S(2)}, u32[]{:S(2)}) collective-permute-start(bf16[1,96,896]{2,1,0:T(8,128)(2,1)} %bitcast.46), channel_id=1, source_target_pairs={{0,4},{1,3},{2,6},{3,1},{4,0},{5,7},{6,2},{7,5},{8,12},{9,11},{10,... | collective-permute-start | bytes 516104 | tf_op jit(solution)/shard_map/ppermute | solution.py:176
  5.2 1.6 %collective-permute-start.4 = (bf16[1,96,896]{2,1,0:T(8,128)(2,1)}, bf16[1,96,896]{2,1,0:T(8,128)(2,1)S(1)}, u32[]{:S(2)}, u32[]{:S(2)}) collective-permute-start(bf16[1,96,896]{2,1,0:T(8,128)(2,1)} %bitcast.47), channel_id=1, source_target_pairs={{0,8},{1,9},{2,10},{3,11},{4,12},{5,13},{6,14},{7,15},{8,0},{9,1},... | collective-permute-start | bytes 516104 | tf_op jit(solution)/shard_map/ppermute | solution.py:176
  6.8 0.7 broadcast_minimum_fusion
  7.4 0.1 reshape.125
  7.6 0.1 reshape.126
  7.6 0.7 broadcast_select_fusion
  8.3 0.1 reshape.127
  8.4 0.1 rev.19
  8.5 0.1 reshape.128
  8.6 0.1 rev.20
  8.7 0.1 stack.63.info
  8.9 0.2 stack.128.info
  9.0 0.0 collective-permute-done
  9.1 1.0 collective-permute-start.2
  10.1 2.7 %collective-permute-start.9 = (bf16[1,96,896]{2,1,0:T(8,128)(2,1)}, bf16[1,96,896]{2,1,0:T(8,128)(2,1)S(1)}, u32[]{:S(2)}, u32[]{:S(2)}) collective-permute-start(bf16[1,96,896]{2,1,0:T(8,128)(2,1)} %bitcast.48), channel_id=1, source_target_pairs={{0,16},{1,17},{2,18},{3,19},{4,20},{5,21},{6,22},{7,23},{8,24},{9,... | collective-permute-start | bytes 516104 | tf_op jit(solution)/shard_map/ppermute | solution.py:176
  12.8 0.0 collective-permute-done.4
  12.8 1.5 %collective-permute-start.5 = (bf16[1,96,896]{2,1,0:T(8,128)(2,1)S(1)}, bf16[1,96,896]{2,1,0:T(8,128)(2,1)S(1)}, u32[]{:S(2)}, u32[]{:S(2)}) collective-permute-start(bf16[1,96,896]{2,1,0:T(8,128)(2,1)S(1)} %collective-permute-done.4), channel_id=1, source_target_pairs={{0,2},{1,5},{2,0},{3,7},{4,6},{5,1},{6,4},{7,3},{8,10},{9,13},{10,... | collective-permute-start | bytes 516104 | tf_op jit(solution)/shard_map/ppermute | solution.py:176
  14.3 1.4 %collective-permute-start.6 = (bf16[1,96,896]{2,1,0:T(8,128)(2,1)S(1)}, bf16[1,96,896]{2,1,0:T(8,128)(2,1)S(1)}, u32[]{:S(2)}, u32[]{:S(2)}) collective-permute-start(bf16[1,96,896]{2,1,0:T(8,128)(2,1)S(1)} %collective-permute-done.4), channel_id=1, source_target_pairs={{0,4},{1,3},{2,6},{3,1},{4,0},{5,7},{6,2},{7,5},{8,12},{9,11},{10,... | collective-permute-start | bytes 516104 | tf_op jit(solution)/shard_map/ppermute | solution.py:176
  15.7 0.0 collective-permute-done.1
  15.7 0.0 collective-permute-done.2
  15.8 1.0 pad_maximum_fusion.refs_0_
  16.8 0.1 collective-permute-start.3
  16.9 1.4 %collective-permute-done.5 = bf16[1,96,896]{2,1,0:T(8,128)(2,1)S(1)} collective-permute-done((bf16[1,96,896]{2,1,0:T(8,128)(2,1)S(1)}, bf16[1,96,896]{2,1,0:T(8,128)(2,1)S(1)}, u32[]{:S(2)}, u32[]{:S(2)}) %collective-permute-start.5) | collective-permute-done | bytes 172064 | tf_op jit(solution)/shard_map/ppermute | solution.py:176
  18.2 1.3 %collective-permute-start.7 = (bf16[1,96,896]{2,1,0:T(8,128)(2,1)S(1)}, bf16[1,96,896]{2,1,0:T(8,128)(2,1)S(1)}, u32[]{:S(2)}, u32[]{:S(2)}) collective-permute-start(bf16[1,96,896]{2,1,0:T(8,128)(2,1)S(1)} %collective-permute-done.5), channel_id=1, source_target_pairs={{0,4},{1,3},{2,6},{3,1},{4,0},{5,7},{6,2},{7,5},{8,12},{9,11},{10,... | collective-permute-start | bytes 516104 | tf_op jit(solution)/shard_map/ppermute | solution.py:176
  19.6 0.2 collective-permute-done.6
  19.8 3.8 %collective-permute-done.7 = bf16[1,96,896]{2,1,0:T(8,128)(2,1)S(1)} collective-permute-done((bf16[1,96,896]{2,1,0:T(8,128)(2,1)S(1)}, bf16[1,96,896]{2,1,0:T(8,128)(2,1)S(1)}, u32[]{:S(2)}, u32[]{:S(2)}) %collective-permute-start.7) | collective-permute-done | bytes 172064 | tf_op jit(solution)/shard_map/ppermute | solution.py:176
  23.7 0.1 collective-permute-start.8
  23.8 2.2 %collective-permute-start.10 = (bf16[1,96,896]{2,1,0:T(8,128)(2,1)}, bf16[1,96,896]{2,1,0:T(8,128)(2,1)S(1)}, u32[]{:S(2)}, u32[]{:S(2)}) collective-permute-start(bf16[1,96,896]{2,1,0:T(8,128)(2,1)} %bitcast.50), channel_id=1, source_target_pairs={{0,24},{1,25},{2,26},{3,27},{4,28},{5,29},{6,30},{7,31},{8,16},{9,... | collective-permute-start | bytes 516104 | tf_op jit(solution)/shard_map/ppermute | solution.py:176
  26.0 6.6 %collective-permute-done.10 = bf16[1,96,896]{2,1,0:T(8,128)(2,1)S(1)} collective-permute-done((bf16[1,96,896]{2,1,0:T(8,128)(2,1)}, bf16[1,96,896]{2,1,0:T(8,128)(2,1)S(1)}, u32[]{:S(2)}, u32[]{:S(2)}) %collective-permute-start.10) | collective-permute-done | bytes 172064 | tf_op jit(solution)/shard_map/ppermute | solution.py:176
  32.7 1.6 %collective-permute-start.11 = (bf16[2,96,896]{2,1,0:T(8,128)(2,1)S(1)}, bf16[2,96,896]{2,1,0:T(8,128)(2,1)S(1)}, u32[]{:S(2)}, u32[]{:S(2)}) collective-permute-start(bf16[2,96,896]{2,1,0:T(8,128)(2,1)S(1)} %constant_dynamic-update-slice_fusion.4.refs_2_), channel_id=1, source_target_pairs={{0,2},{1,3},{2,0},{3,1},{4,6},{5,7},{6,4},{7,5},{8,10},{9,11},{10,... | collective-permute-start | bytes 1032200 | tf_op jit(solution)/shard_map/ppermute | solution.py:176
  34.2 1.3 %collective-permute-start.12 = (bf16[2,96,896]{2,1,0:T(8,128)(2,1)S(1)}, bf16[2,96,896]{2,1,0:T(8,128)(2,1)S(1)}, u32[]{:S(2)}, u32[]{:S(2)}) collective-permute-start(bf16[2,96,896]{2,1,0:T(8,128)(2,1)S(1)} %constant_dynamic-update-slice_fusion.4.refs_2_), channel_id=1, source_target_pairs={{0,4},{1,5},{2,6},{3,7},{4,0},{5,1},{6,2},{7,3},{8,12},{9,13},{10,... | collective-permute-start | bytes 1032200 | tf_op jit(solution)/shard_map/ppermute | solution.py:176
  35.5 0.7 collective-permute-start.13
  36.2 0.7 convert_element_type.5
  36.9 6.8 %collective-permute-done.11.refs_3_ = bf16[2,96,896]{2,1,0:T(8,128)(2,1)S(1)} collective-permute-done((bf16[2,96,896]{2,1,0:T(8,128)(2,1)S(1)}, bf16[2,96,896]{2,1,0:T(8,128)(2,1)S(1)}, u32[]{:S(2)}, u32[]{:S(2)}) %collective-permute-start.11) | collective-permute-done | bytes 344096 | tf_op jit(solution)/shard_map/ppermute | solution.py:176
  43.7 0.0 collective-permute-start.14
  43.7 7.1 %collective-permute-done.12.refs_4_ = bf16[2,96,896]{2,1,0:T(8,128)(2,1)S(1)} collective-permute-done((bf16[2,96,896]{2,1,0:T(8,128)(2,1)S(1)}, bf16[2,96,896]{2,1,0:T(8,128)(2,1)S(1)}, u32[]{:S(2)}, u32[]{:S(2)}) %collective-permute-start.12) | collective-permute-done | bytes 344096 | tf_op jit(solution)/shard_map/ppermute | solution.py:176
  50.8 0.0 collective-permute-start.15
  50.8 0.5 collective-permute-start.16
  51.3 0.1 collective-permute-start.17
  51.4 14.2 %row_stats.2 = f32[3,256]{1,0:T(4,128)S(1)} custom-call(s32[37]{0:T(128)S(1)} %stack.63.info, s32[8,256]{1,0:T(8,128)S(1)} %broadcast_in_dim.32.limits, bf16[4752,3584]{1,0:T(8,128)(2,1)} %bitcast.43, bf16[4,96,896]{2,1,0:T(8,128)(2,1)S(1)} %pad_maximum_fusion.refs_0_, bf16[4,96,896]{2,1,0:T(8,128)(2,1)S(1)} %collective-permute-done.3.refs_1_, ...), custom_call_target="tpu_custom_call" | custom-call | flops 8719958016 | bytes 34062336 | tf_op jit(solution)/shard_map/row_stats/pallas_call | solution.py:110
  65.6 0.0 copy-start.1
  65.6 24.3 %row_stats.3 = f32[3,512]{1,0:T(4,128)S(1)} custom-call(s32[73]{0:T(128)S(1)} %stack.128.info, s32[8,512]{1,0:T(8,128)S(1)} %broadcast_in_dim.33.limits, bf16[4752,3584]{1,0:T(8,128)(2,1)} %bitcast.44, bf16[4,96,896]{2,1,0:T(8,128)(2,1)S(1)} %constant_dynamic-update-slice_fusion.refs_2_.refs_0_, ...), custom_call_target="tpu_custom_call" | custom-call | flops 17439916032 | bytes 34062336 | tf_op jit(solution)/shard_map/row_stats/pallas_call | solution.py:110
  90.0 5.2 %all-gather.1 = f32[4,3,768]{2,1,0:T(4,128)S(1)} all-gather(f32[1,3,768]{2,1,0:T(4,128)S(1)} %maximum_bitcast_fusion), channel_id=2, replica_groups=mesh['seq'=8,'vocab'=4] {'vocab'}, dimensions={0}, use_global_device_ids=true | all-gather | bytes 46080 | tf_op jit(solution)/shard_map/all_gather | solution.py:292
  95.3 0.1 stack.129
  95.4 0.1 stack.130
  95.4 0.1 stack.134
  95.5 0.1 stack.131
  95.6 0.1 stack.135
  95.7 0.1 stack.133
  95.8 0.1 reshape.131
  95.9 0.1 reshape.133
  96.0 0.1 rev.22
  96.2 0.1 reshape.132
  96.3 0.1 reshape.135
  96.3 0.1 reshape.136
  96.5 0.1 rev.23
  96.7 0.7 broadcast_in_dim.35
  97.3 5.5 %all-to-all-start = ((f32[8,4,768]{2,1,0:T(4,128)}), f32[8,4,768]{2,1,0:T(4,128)S(1)}, u32[]{:S(2)}, u32[]{:S(2)}) async-start(f32[8,4,768]{2,1,0:T(4,128)} %broadcast_in_dim.35), calls=%async_computation | async-start | bytes 196608 | tf_op jit(solution)/shard_map/all_to_all | solution.py:296
  102.8 0.6 broadcast_in_dim.36.owner
  103.4 0.6 broadcast_in_dim.37.place
  104.0 5.9 %all-to-all-done.parts = f32[8,4,768]{2,1,0:T(4,128)S(1)} async-done(((f32[8,4,768]{2,1,0:T(4,128)}), f32[8,4,768]{2,1,0:T(4,128)S(1)}, u32[]{:S(2)}, u32[]{:S(2)}) %all-to-all-start) | async-done | bytes 98336 | tf_op jit(solution)/shard_map/all_to_all | solution.py:296
  109.9 0.6 copy-done
  110.6 1.7 %finish.1 = (f32[1,96]{1,0:T(1,128)}, f32[1,1]{1,0:T(1,128)}) custom-call(s32[1]{0:T(128)} %bitcast.own, f32[8,4,768]{2,1,0:T(4,128)} %copy-done, s32[1,768]{1,0:T(1,128)} %broadcast_in_dim.36.owner, s32[1,768]{1,0:T(1,128)} %broadcast_in_dim.37.place), custom_call_target="tpu_custom_call" | custom-call | tf_op jit(solution)/shard_map/finish/pallas_call | solution.py:161
  (44 shorter events, 0.5 us)
Async XLA Ops:
  0.6 8.4 %collective-permute-start = (bf16[1,96,896]{2,1,0:T(8,128)(2,1)}, bf16[1,96,896]{2,1,0:T(8,128)(2,1)S(1)}, u32[]{:S(2)}, u32[]{:S(2)}) collective-permute-start(bf16[1,96,896]{2,1,0:T(8,128)(2,1)} %bitcast.45), channel_id=1, source_target_pairs={{0,2},{1,5},{2,0},{3,7},{4,6},{5,1},{6,4},{7,3},{8,10},{9,13},{10,... | collective-permute-start | bytes 516104 | tf_op jit(solution)/shard_map/ppermute | solution.py:176
  3.7 12.1 %collective-permute-start.1 = (bf16[1,96,896]{2,1,0:T(8,128)(2,1)}, bf16[1,96,896]{2,1,0:T(8,128)(2,1)S(1)}, u32[]{:S(2)}, u32[]{:S(2)}) collective-permute-start(bf16[1,96,896]{2,1,0:T(8,128)(2,1)} %bitcast.46), channel_id=1, source_target_pairs={{0,4},{1,3},{2,6},{3,1},{4,0},{5,7},{6,2},{7,5},{8,12},{9,11},{10,... | collective-permute-start | bytes 516104 | tf_op jit(solution)/shard_map/ppermute | solution.py:176
  5.2 7.7 %collective-permute-start.4 = (bf16[1,96,896]{2,1,0:T(8,128)(2,1)}, bf16[1,96,896]{2,1,0:T(8,128)(2,1)S(1)}, u32[]{:S(2)}, u32[]{:S(2)}) collective-permute-start(bf16[1,96,896]{2,1,0:T(8,128)(2,1)} %bitcast.47), channel_id=1, source_target_pairs={{0,8},{1,9},{2,10},{3,11},{4,12},{5,13},{6,14},{7,15},{8,0},{9,1},... | collective-permute-start | bytes 516104 | tf_op jit(solution)/shard_map/ppermute | solution.py:176
  9.1 6.7 %collective-permute-start.2 = (bf16[1,96,896]{2,1,0:T(8,128)(2,1)S(1)}, bf16[1,96,896]{2,1,0:T(8,128)(2,1)S(1)}, u32[]{:S(2)}, u32[]{:S(2)}) collective-permute-start(bf16[1,96,896]{2,1,0:T(8,128)(2,1)S(1)} %collective-permute-done), channel_id=1, source_target_pairs={{0,4},{1,3},{2,6},{3,1},{4,0},{5,7},{6,2},{7,5},{8,12},{9,11},{10,... | collective-permute-start | bytes 516104 | tf_op jit(solution)/shard_map/ppermute | solution.py:176
  10.1 15.9 %collective-permute-start.9 = (bf16[1,96,896]{2,1,0:T(8,128)(2,1)}, bf16[1,96,896]{2,1,0:T(8,128)(2,1)S(1)}, u32[]{:S(2)}, u32[]{:S(2)}) collective-permute-start(bf16[1,96,896]{2,1,0:T(8,128)(2,1)} %bitcast.48), channel_id=1, source_target_pairs={{0,16},{1,17},{2,18},{3,19},{4,20},{5,21},{6,22},{7,23},{8,24},{9,... | collective-permute-start | bytes 516104 | tf_op jit(solution)/shard_map/ppermute | solution.py:176
  12.8 5.4 %collective-permute-start.5 = (bf16[1,96,896]{2,1,0:T(8,128)(2,1)S(1)}, bf16[1,96,896]{2,1,0:T(8,128)(2,1)S(1)}, u32[]{:S(2)}, u32[]{:S(2)}) collective-permute-start(bf16[1,96,896]{2,1,0:T(8,128)(2,1)S(1)} %collective-permute-done.4), channel_id=1, source_target_pairs={{0,2},{1,5},{2,0},{3,7},{4,6},{5,1},{6,4},{7,3},{8,10},{9,13},{10,... | collective-permute-start | bytes 516104 | tf_op jit(solution)/shard_map/ppermute | solution.py:176
  14.3 5.5 %collective-permute-start.6 = (bf16[1,96,896]{2,1,0:T(8,128)(2,1)S(1)}, bf16[1,96,896]{2,1,0:T(8,128)(2,1)S(1)}, u32[]{:S(2)}, u32[]{:S(2)}) collective-permute-start(bf16[1,96,896]{2,1,0:T(8,128)(2,1)S(1)} %collective-permute-done.4), channel_id=1, source_target_pairs={{0,4},{1,3},{2,6},{3,1},{4,0},{5,7},{6,2},{7,5},{8,12},{9,11},{10,... | collective-permute-start | bytes 516104 | tf_op jit(solution)/shard_map/ppermute | solution.py:176
  16.8 34.5 %collective-permute-start.3 = (bf16[4,96,896]{2,1,0:T(8,128)(2,1)S(1)}, bf16[4,96,896]{2,1,0:T(8,128)(2,1)S(1)}, u32[]{:S(2)}, u32[]{:S(2)}) collective-permute-start(bf16[4,96,896]{2,1,0:T(8,128)(2,1)S(1)} %pad_maximum_fusion.refs_0_), channel_id=1, source_target_pairs={{0,1},{1,0},{2,3},{3,2},{4,5},{5,4},{6,7},{7,6},{8,9},{9,8},{10,11... | collective-permute-start | bytes 2064392 | tf_op jit(solution)/shard_map/ppermute | solution.py:176
  18.2 5.4 %collective-permute-start.7 = (bf16[1,96,896]{2,1,0:T(8,128)(2,1)S(1)}, bf16[1,96,896]{2,1,0:T(8,128)(2,1)S(1)}, u32[]{:S(2)}, u32[]{:S(2)}) collective-permute-start(bf16[1,96,896]{2,1,0:T(8,128)(2,1)S(1)} %collective-permute-done.5), channel_id=1, source_target_pairs={{0,4},{1,3},{2,6},{3,1},{4,0},{5,7},{6,2},{7,5},{8,12},{9,11},{10,... | collective-permute-start | bytes 516104 | tf_op jit(solution)/shard_map/ppermute | solution.py:176
  23.7 27.7 %collective-permute-start.8 = (bf16[4,96,896]{2,1,0:T(8,128)(2,1)S(1)}, bf16[4,96,896]{2,1,0:T(8,128)(2,1)S(1)}, u32[]{:S(2)}, u32[]{:S(2)}) collective-permute-start(bf16[4,96,896]{2,1,0:T(8,128)(2,1)S(1)} %constant_dynamic-update-slice_fusion.refs_2_.refs_0_), channel_id=1, source_target_pairs={{0,1},{1,0},{2,3},{3,2},{4,5},{5,4},{6,7},{7,6},{8,9},{9,8},{10,11... | collective-permute-start | bytes 2064392 | tf_op jit(solution)/shard_map/ppermute | solution.py:176
  23.8 8.9 %collective-permute-start.10 = (bf16[1,96,896]{2,1,0:T(8,128)(2,1)}, bf16[1,96,896]{2,1,0:T(8,128)(2,1)S(1)}, u32[]{:S(2)}, u32[]{:S(2)}) collective-permute-start(bf16[1,96,896]{2,1,0:T(8,128)(2,1)} %bitcast.50), channel_id=1, source_target_pairs={{0,24},{1,25},{2,26},{3,27},{4,28},{5,29},{6,30},{7,31},{8,16},{9,... | collective-permute-start | bytes 516104 | tf_op jit(solution)/shard_map/ppermute | solution.py:176
  32.7 11.0 %collective-permute-start.11 = (bf16[2,96,896]{2,1,0:T(8,128)(2,1)S(1)}, bf16[2,96,896]{2,1,0:T(8,128)(2,1)S(1)}, u32[]{:S(2)}, u32[]{:S(2)}) collective-permute-start(bf16[2,96,896]{2,1,0:T(8,128)(2,1)S(1)} %constant_dynamic-update-slice_fusion.4.refs_2_), channel_id=1, source_target_pairs={{0,2},{1,3},{2,0},{3,1},{4,6},{5,7},{6,4},{7,5},{8,10},{9,11},{10,... | collective-permute-start | bytes 1032200 | tf_op jit(solution)/shard_map/ppermute | solution.py:176
  34.2 16.6 %collective-permute-start.12 = (bf16[2,96,896]{2,1,0:T(8,128)(2,1)S(1)}, bf16[2,96,896]{2,1,0:T(8,128)(2,1)S(1)}, u32[]{:S(2)}, u32[]{:S(2)}) collective-permute-start(bf16[2,96,896]{2,1,0:T(8,128)(2,1)S(1)} %constant_dynamic-update-slice_fusion.4.refs_2_), channel_id=1, source_target_pairs={{0,4},{1,5},{2,6},{3,7},{4,0},{5,1},{6,2},{7,3},{8,12},{9,13},{10,... | collective-permute-start | bytes 1032200 | tf_op jit(solution)/shard_map/ppermute | solution.py:176
  35.5 15.3 %collective-permute-start.13 = (bf16[2,96,896]{2,1,0:T(8,128)(2,1)S(1)}, bf16[2,96,896]{2,1,0:T(8,128)(2,1)S(1)}, u32[]{:S(2)}, u32[]{:S(2)}) collective-permute-start(bf16[2,96,896]{2,1,0:T(8,128)(2,1)S(1)} %constant_dynamic-update-slice_fusion.4.refs_2_), channel_id=1, source_target_pairs={{0,6},{1,7},{2,4},{3,5},{4,2},{5,3},{6,0},{7,1},{8,14},{9,15},{10,... | collective-permute-start | bytes 1032200 | tf_op jit(solution)/shard_map/ppermute | solution.py:176
  43.7 21.9 %collective-permute-start.14 = (bf16[2,96,896]{2,1,0:T(8,128)(2,1)S(1)}, bf16[2,96,896]{2,1,0:T(8,128)(2,1)S(1)}, u32[]{:S(2)}, u32[]{:S(2)}) collective-permute-start(bf16[2,96,896]{2,1,0:T(8,128)(2,1)S(1)} %constant_dynamic-update-slice_fusion.4.refs_2_), channel_id=1, source_target_pairs={{0,1},{1,0},{2,3},{3,2},{4,5},{5,4},{6,7},{7,6},{8,9},{9,8},{10,11... | collective-permute-start | bytes 1032200 | tf_op jit(solution)/shard_map/ppermute | solution.py:176
  50.8 14.8 %collective-permute-start.15 = (bf16[2,96,896]{2,1,0:T(8,128)(2,1)S(1)}, bf16[2,96,896]{2,1,0:T(8,128)(2,1)S(1)}, u32[]{:S(2)}, u32[]{:S(2)}) collective-permute-start(bf16[2,96,896]{2,1,0:T(8,128)(2,1)S(1)} %collective-permute-done.11.refs_3_), channel_id=1, source_target_pairs={{0,1},{1,0},{2,3},{3,2},{4,5},{5,4},{6,7},{7,6},{8,9},{9,8},{10,11... | collective-permute-start | bytes 1032200 | tf_op jit(solution)/shard_map/ppermute | solution.py:176
  50.8 14.8 %collective-permute-start.16 = (bf16[2,96,896]{2,1,0:T(8,128)(2,1)S(1)}, bf16[2,96,896]{2,1,0:T(8,128)(2,1)S(1)}, u32[]{:S(2)}, u32[]{:S(2)}) collective-permute-start(bf16[2,96,896]{2,1,0:T(8,128)(2,1)S(1)} %collective-permute-done.12.refs_4_), channel_id=1, source_target_pairs={{0,1},{1,0},{2,3},{3,2},{4,5},{5,4},{6,7},{7,6},{8,9},{9,8},{10,11... | collective-permute-start | bytes 1032200 | tf_op jit(solution)/shard_map/ppermute | solution.py:176
  51.3 14.3 %collective-permute-start.17 = (bf16[2,96,896]{2,1,0:T(8,128)(2,1)S(1)}, bf16[2,96,896]{2,1,0:T(8,128)(2,1)S(1)}, u32[]{:S(2)}, u32[]{:S(2)}) collective-permute-start(bf16[2,96,896]{2,1,0:T(8,128)(2,1)S(1)} %collective-permute-done.13.refs_5_), channel_id=1, source_target_pairs={{0,1},{1,0},{2,3},{3,2},{4,5},{5,4},{6,7},{7,6},{8,9},{9,8},{10,11... | collective-permute-start | bytes 1032200 | tf_op jit(solution)/shard_map/ppermute | solution.py:176
  65.6 37.3 %copy-start.1 = (s32[768]{0:T(1024)S(1)}, s32[768]{0:T(1024)}, u32[]{:S(2)}) copy-start(s32[768]{0:T(1024)} %param.7) | copy-start | bytes 9220
  97.3 12.6 %all-to-all-start = ((f32[8,4,768]{2,1,0:T(4,128)}), f32[8,4,768]{2,1,0:T(4,128)S(1)}, u32[]{:S(2)}, u32[]{:S(2)}) async-start(f32[8,4,768]{2,1,0:T(4,128)} %broadcast_in_dim.35), calls=%async_computation | async-start | bytes 196608 | tf_op jit(solution)/shard_map/all_to_all | solution.py:296
  109.9 0.6 copy-start

commit v3 on v2

--- a/solution.py
+++ b/solution.py
@@ -42,7 +42,7 @@
         moment[:, lanes] = moments[0] + moments[1]
 
 
-def stats_kernel(half, steps, slots, moves, info, limits, w_hbm, *refs):
+def stats_kernel(half, steps, slots, paired, moves, info, limits, w_hbm, *refs):
     arrays, (out, lhs, w_buf, sem, buf0, buf1, peak, total, moment) = refs[:-9], refs[-9:]
     tile = 2 * half
     first = info[0]
@@ -67,25 +67,52 @@
     peak[...] = jnp.full_like(peak, NEG)
     total[...] = jnp.zeros_like(total)
     moment[...] = jnp.zeros_like(moment)
-    buf1[...] = jnp.zeros_like(buf1)
-
-    def body(step, carry):
-        slot = lax.rem(step, slots)
+
+    def arrive(step):
         copy(step).wait()
-
-        @pl.when(step + slots - 1 < steps)
-        def _():
-            copy(step + slots - 1).start()
-
-        base = first + step * tile
-        buf0[...] = dot_t(w_buf[slot, :half, :], lhs[...])
-        fold(buf1, half, limits, jnp.where(step == 0, FAR, base - half), peak, total, moment)
-        buf1[...] = dot_t(w_buf[slot, half:, :], lhs[...])
-        fold(buf0, half, limits, base, peak, total, moment)
-        return carry
-
-    lax.fori_loop(0, steps, body, 0)
-    fold(buf1, half, limits, first + steps * tile - half, peak, total, moment)
+        if isinstance(step, int):
+            if step + slots - 1 < steps:
+                copy(step + slots - 1).start()
+        else:
+
+            @pl.when(step + slots - 1 < steps)
+            def _():
+                copy(step + slots - 1).start()
+
+        return step % slots if isinstance(step, int) else lax.rem(step, slots)
+
+    if paired:
+        buf0[...] = dot_t(w_buf[arrive(0)], lhs[...])
+
+        def body(pair, carry):
+            step = 2 * pair
+            buf1[...] = dot_t(w_buf[arrive(step + 1)], lhs[...])
+            fold(buf0, tile, limits, first + step * tile, peak, total, moment)
+            buf0[...] = dot_t(w_buf[arrive(step + 2)], lhs[...])
+            fold(buf1, tile, limits, first + (step + 1) * tile, peak, total, moment)
+            return carry
+
+        lax.fori_loop(0, (steps - 1) // 2, body, 0)
+        last = (steps - 1) // 2 * 2
+        if last + 1 < steps:
+            buf1[...] = dot_t(w_buf[arrive(last + 1)], lhs[...])
+        fold(buf0, tile, limits, first + last * tile, peak, total, moment)
+        if last + 1 < steps:
+            fold(buf1, tile, limits, first + (last + 1) * tile, peak, total, moment)
+    else:
+        buf1[...] = jnp.zeros_like(buf1)
+
+        def body(step, carry):
+            slot = arrive(step)
+            base = first + step * tile
+            buf0[...] = dot_t(w_buf[slot, :half, :], lhs[...])
+            fold(buf1, half, limits, jnp.where(step == 0, FAR, base - half), peak, total, moment)
+            buf1[...] = dot_t(w_buf[slot, half:, :], lhs[...])
+            fold(buf0, half, limits, base, peak, total, moment)
+            return carry
+
+        lax.fori_loop(0, steps, body, 0)
+        fold(buf1, half, limits, first + steps * tile - half, peak, total, moment)
     top = jnp.max(peak[...], axis=0, keepdims=True)
     drop = peak[...] - top
     ratio = jnp.exp(drop)
@@ -107,8 +134,10 @@
     fixed = tuple((m[0], m[2], m[3], m[4] if isinstance(m[4], int) else None) for m in moves)
     wide = half * 2 * steps
     slots = max(2, min(4, steps))
+    paired = tokens > 256
+    height = 2 * half if paired else half
     return pl.pallas_call(
-        functools.partial(stats_kernel, half, steps, slots, fixed),
+        functools.partial(stats_kernel, half, steps, slots, paired, fixed),
         out_shape=jax.ShapeDtypeStruct((3, tokens), jnp.float32),
         in_specs=[pl.BlockSpec(memory_space=pltpu.SMEM), pl.BlockSpec(memory_space=pltpu.VMEM), pl.BlockSpec(memory_space=pl.ANY)]
         + [pl.BlockSpec(memory_space=pltpu.VMEM)] * len(arrays),
@@ -117,8 +146,8 @@
             pltpu.VMEM((tokens, depth), jnp.bfloat16),
             pltpu.VMEM((slots, 2 * half, depth), jnp.bfloat16),
             pltpu.SemaphoreType.DMA((slots,)),
-            pltpu.VMEM((half, tokens), jnp.float32),
-            pltpu.VMEM((half, tokens), jnp.float32),
+            pltpu.VMEM((height, tokens), jnp.float32),
+            pltpu.VMEM((height, tokens), jnp.float32),
             pltpu.VMEM((8, tokens), jnp.float32),
             pltpu.VMEM((8, tokens), jnp.float32),
             pltpu.VMEM((8, tokens), jnp.float32),
@@ -136,6 +165,36 @@
     drop = parts[:, 0] - top[None]
     ratio = jnp.exp(drop)
     return top, jnp.sum(ratio * parts[:, 1], axis=0), jnp.sum(ratio * (parts[:, 2] + parts[:, 1] * drop), axis=0)
+
+
+def combine_kernel(groups, own, parts, mask, out):
+    tokens = parts.shape[2]
+    stats = list(merge(parts[...]))
+    stats = jnp.stack([*stats, stats[0]])
+    lane = lax.broadcasted_iota(jnp.int32, stats.shape, 1)
+    width = tokens // groups
+    bit = 1
+    while bit < groups:
+        step = bit * width
+        low = lax.rem(lane // step, 2) == 0
+        flipped = jnp.where(low, pltpu.roll(stats, tokens - step, 1), pltpu.roll(stats, step, 1))
+        stats = jnp.where((own[0] & bit) != 0, flipped, stats)
+        bit *= 2
+    row = lax.broadcasted_iota(jnp.int32, stats.shape, 0)
+    stats = jnp.where(row == 3, mask[...], stats)
+    for g in range(groups):
+        out[g] = stats
+
+
+def combine(groups, own, parts, mask):
+    tokens = parts.shape[2]
+    return pl.pallas_call(
+        functools.partial(combine_kernel, groups),
+        out_shape=jax.ShapeDtypeStruct((groups, 4, tokens), jnp.float32),
+        in_specs=[pl.BlockSpec(memory_space=pltpu.SMEM)] + [pl.BlockSpec(memory_space=pltpu.VMEM)] * 2,
+        out_specs=pl.BlockSpec(memory_space=pltpu.VMEM),
+        name="combine",
+    )(own, parts, mask)
 
 
 def finish_kernel(own, parts, owner, place, entropy_out, mean_out):
@@ -212,7 +271,8 @@
                 if cut:
                     early.append((2 + side, index, 0, cut, row, column))
                 if cut < rows:
-                    late.append((side, index, cut, rows - cut, row + cut - ready, column))
+                    source = (10 + side, 0) if i and j else (side, index)
+                    late.append((source[0], source[1], cut, rows - cut, row + cut - ready, column))
         for part in range(4):
             j, i = ((0, 0), (0, 1), (1, 0), (1, 1))[part]
             for k in range(seq // 2 - 2):
@@ -235,8 +295,9 @@
     near_d = swap(near_x, y_or_x)
     mine = jnp.concatenate([own, own_x, own_w, own_d], axis=0)
     theirs = swap(mine, cores)
-    near_mine = jnp.concatenate([near, near_x, near_w, near_d], axis=0)
+    near_mine = jnp.concatenate([near, near_x, near_w], axis=0)
     near_theirs = swap(near_mine, cores)
+    near_theirs_d = swap(near_d, cores)
     far_parts = [jnp.concatenate(far, axis=0)]
     for move in (both(0, 2), both(1, 0), both(1, 2)):
         far_parts.append(swap(far_parts[0], move))
@@ -247,7 +308,7 @@
     done = row_stats(
         early_info, early_limits, [mine, theirs, near_mine, near_theirs], early, w_rows, half, steps, 30 * 2**20
     )
-    arrays = [near_mine, near_theirs, *far_parts, *far_theirs]
+    arrays = [near_mine, near_theirs, *far_parts, *far_theirs, near_d, near_theirs_d]
     rest = row_stats(late_info, late_limits, arrays, late, w_rows, half, steps, 30 * 2**20)
     return jnp.concatenate([done, rest], axis=1)
 
@@ -289,12 +350,11 @@
         )
         stats = xor_blocks(stats, seq, my_seq)
 
-    top, total, moment = merge(lax.all_gather(stats, "vocab"))
-    mask = jnp.pad(loss_mask.astype(jnp.float32), (0, tokens - each))
-    sent = xor_blocks(jnp.stack([top, total, moment]), seq, my_seq)
-    sent = jnp.concatenate([sent, mask[None]], axis=0)
-    parts = lax.all_to_all(jnp.broadcast_to(sent[None], (seq, 4, tokens)), "seq", 0, 0, tiled=True)
-    entropy, mean = finish(my_seq[None].astype(jnp.int32), parts, (positions // each)[None], (positions % each)[None], each)
+    own = my_seq[None].astype(jnp.int32)
+    mask = jnp.pad(loss_mask.astype(jnp.float32), (0, tokens - each))[None]
+    sent = combine(seq, own, lax.all_gather(stats, "vocab"), mask)
+    parts = lax.all_to_all(sent, "seq", 0, 0, tiled=True)
+    entropy, mean = finish(own, parts, (positions // each)[None], (positions % each)[None], each)
     return entropy.reshape(each), mean.reshape(())
 
 

time: 113 us -> 108 us (0.956)
  starting transfers between devices: 26.1 us -> 21.9 us
  local copies, waits for them, and re-layouts: 4.66 us -> 3.33 us
    ppermute x18 -> x19, starting transfers between devices: 20.6 us -> 16.8 us  [permute(): return lax.ppermute(array, AXES, pairs)]
    ppermute x18 -> x19, waiting for transfers between devices: 26 us -> 26.3 us  [permute(): return lax.ppermute(array, AXES, pairs)]
    pallas_call x2 -> x3, Pallas kernels: 38.5 us -> 38.6 us  [the longest x2 37 us: row_stats(): pl.pallas_call(functools.partial(stats_kernel, half, steps, slots, paired...]
  transfers between devices with their start and end apart: 19 -> 20, of which waited for: 7 -> 6; matrix products, arithmetic and copies ran while one was open for 5% -> 5% of each run, Pallas kernels for 13% -> 21%
where the time goes in v3:
time: 108 us; the launch traced here: 107 us
  Pallas kernels  40.3 us (37%)
  waiting for transfers between devices  32.2 us (30%)
  starting transfers between devices  21.9 us (20%)
  blocking collectives  5.67 us (5%)
  local copies, waits for them, and re-layouts  3.33 us (3%)
  other arithmetic  3.09 us (3%)
    pallas_call x2, Pallas kernels, row_stats(): pl.pallas_call(functools.partial(stats_kernel, half, steps, slots, paired...  37 us
    ppermute x19, waiting for transfers between devices, permute(): return lax.ppermute(array, AXES, pairs)  26.3 us
    ppermute x19, starting transfers between devices, permute(): return lax.ppermute(array, AXES, pairs)  16.8 us
    all_to_all x1, waiting for transfers between devices, local(): parts = lax.all_to_all(sent, 'seq', 0, 0, tiled=True)  5.92 us
    all_gather x1, blocking collectives, local(): sent = combine(seq, own, lax.all_gather(stats, 'vocab'), mask)  5.67 us
    all_to_all x1, starting transfers between devices, local(): parts = lax.all_to_all(sent, 'seq', 0, 0, tiled=True)  5.15 us
  transfers between devices with their start and end apart: 20, of which 6 were waited for; matrix products, arithmetic and copies ran while one was open for 5% of the time, Pallas kernels for 21%

profile of v3, /device:TPU:0, one launch (start us, length us, event | category | flops | bytes accessed | tf_op | source)
XLA Modules:
  0.0 107.4 jit_solution(16421572766655683429)
XLA Ops:
  0.6 3.0 %collective-permute-start = (bf16[1,96,896]{2,1,0:T(8,128)(2,1)}, bf16[1,96,896]{2,1,0:T(8,128)(2,1)S(1)}, u32[]{:S(2)}, u32[]{:S(2)}) collective-permute-start(bf16[1,96,896]{2,1,0:T(8,128)(2,1)} %bitcast.18), channel_id=1, source_target_pairs={{0,2},{1,5},{2,0},{3,7},{4,6},{5,1},{6,4},{7,3},{8,10},{9,13},{10,... | collective-permute-start | bytes 516104 | tf_op jit(solution)/shard_map/ppermute | solution.py:235
  3.7 1.5 %collective-permute-start.1 = (bf16[1,96,896]{2,1,0:T(8,128)(2,1)}, bf16[1,96,896]{2,1,0:T(8,128)(2,1)S(1)}, u32[]{:S(2)}, u32[]{:S(2)}) collective-permute-start(bf16[1,96,896]{2,1,0:T(8,128)(2,1)} %bitcast.19), channel_id=1, source_target_pairs={{0,4},{1,3},{2,6},{3,1},{4,0},{5,7},{6,2},{7,5},{8,12},{9,11},{10,... | collective-permute-start | bytes 516104 | tf_op jit(solution)/shard_map/ppermute | solution.py:235
  5.2 1.6 %collective-permute-start.4 = (bf16[1,96,896]{2,1,0:T(8,128)(2,1)}, bf16[1,96,896]{2,1,0:T(8,128)(2,1)S(1)}, u32[]{:S(2)}, u32[]{:S(2)}) collective-permute-start(bf16[1,96,896]{2,1,0:T(8,128)(2,1)} %bitcast.20), channel_id=1, source_target_pairs={{0,8},{1,9},{2,10},{3,11},{4,12},{5,13},{6,14},{7,15},{8,0},{9,1},... | collective-permute-start | bytes 516104 | tf_op jit(solution)/shard_map/ppermute | solution.py:235
  6.8 2.6 %collective-permute-start.8 = (bf16[1,96,896]{2,1,0:T(8,128)(2,1)}, bf16[1,96,896]{2,1,0:T(8,128)(2,1)S(1)}, u32[]{:S(2)}, u32[]{:S(2)}) collective-permute-start(bf16[1,96,896]{2,1,0:T(8,128)(2,1)} %bitcast.21), channel_id=1, source_target_pairs={{0,16},{1,17},{2,18},{3,19},{4,20},{5,21},{6,22},{7,23},{8,24},{9,... | collective-permute-start | bytes 516104 | tf_op jit(solution)/shard_map/ppermute | solution.py:235
  9.3 0.2 collective-permute-start.9
  9.6 0.7 broadcast_minimum_fusion
  10.3 0.1 reshape.30
  10.4 0.1 reshape.31
  10.5 0.7 broadcast_select_fusion
  11.1 0.1 reshape.32
  11.2 0.1 rev.10
  11.3 0.1 reshape.33
  11.4 0.1 rev.11
  11.6 0.1 stack.31.info
  11.7 0.2 stack.32.info
  11.9 1.3 %collective-permute-done.4 = bf16[1,96,896]{2,1,0:T(8,128)(2,1)S(1)} collective-permute-done((bf16[1,96,896]{2,1,0:T(8,128)(2,1)}, bf16[1,96,896]{2,1,0:T(8,128)(2,1)S(1)}, u32[]{:S(2)}, u32[]{:S(2)}) %collective-permute-start.4) | collective-permute-done | bytes 172064 | tf_op jit(solution)/shard_map/ppermute | solution.py:235
  13.2 0.5 collective-permute-start.5
  13.8 8.6 %collective-permute-done.8 = bf16[1,96,896]{2,1,0:T(8,128)(2,1)S(1)} collective-permute-done((bf16[1,96,896]{2,1,0:T(8,128)(2,1)}, bf16[1,96,896]{2,1,0:T(8,128)(2,1)S(1)}, u32[]{:S(2)}, u32[]{:S(2)}) %collective-permute-start.8) | collective-permute-done | bytes 172064 | tf_op jit(solution)/shard_map/ppermute | solution.py:235
  22.4 0.5 collective-permute-start.6
  22.9 0.0 collective-permute-done.9
  23.0 0.6 collective-permute-start.10
  23.6 0.0 collective-permute-done
  23.6 1.5 %collective-permute-start.11 = (bf16[2,96,896]{2,1,0:T(8,128)(2,1)S(1)}, bf16[2,96,896]{2,1,0:T(8,128)(2,1)S(1)}, u32[]{:S(2)}, u32[]{:S(2)}) collective-permute-start(bf16[2,96,896]{2,1,0:T(8,128)(2,1)S(1)} %constant_dynamic-update-slice_fusion.3.refs_2_), channel_id=1, source_target_pairs={{0,4},{1,5},{2,6},{3,7},{4,0},{5,1},{6,2},{7,3},{8,12},{9,13},{10,... | collective-permute-start | bytes 1032200 | tf_op jit(solution)/shard_map/ppermute | solution.py:235
  25.1 0.0 collective-permute-done.1
  25.1 1.5 %collective-permute-start.12 = (bf16[2,96,896]{2,1,0:T(8,128)(2,1)S(1)}, bf16[2,96,896]{2,1,0:T(8,128)(2,1)S(1)}, u32[]{:S(2)}, u32[]{:S(2)}) collective-permute-start(bf16[2,96,896]{2,1,0:T(8,128)(2,1)S(1)} %constant_dynamic-update-slice_fusion.3.refs_2_), channel_id=1, source_target_pairs={{0,6},{1,7},{2,4},{3,5},{4,2},{5,3},{6,0},{7,1},{8,14},{9,15},{10,... | collective-permute-start | bytes 1032200 | tf_op jit(solution)/shard_map/ppermute | solution.py:235
  26.6 0.0 collective-permute-done.5
  26.6 0.0 collective-permute-start.13
  26.6 4.3 %collective-permute-done.6 = bf16[1,96,896]{2,1,0:T(8,128)(2,1)S(1)} collective-permute-done((bf16[1,96,896]{2,1,0:T(8,128)(2,1)S(1)}, bf16[1,96,896]{2,1,0:T(8,128)(2,1)S(1)}, u32[]{:S(2)}, u32[]{:S(2)}) %collective-permute-start.6) | collective-permute-done | bytes 172064 | tf_op jit(solution)/shard_map/ppermute | solution.py:235
  31.0 0.4 collective-permute-start.2
  31.4 8.8 %collective-permute-done.2 = bf16[1,96,896]{2,1,0:T(8,128)(2,1)S(1)} collective-permute-done((bf16[1,96,896]{2,1,0:T(8,128)(2,1)S(1)}, bf16[1,96,896]{2,1,0:T(8,128)(2,1)S(1)}, u32[]{:S(2)}, u32[]{:S(2)}) %collective-permute-start.2) | collective-permute-done | bytes 172064 | tf_op jit(solution)/shard_map/ppermute | solution.py:235
  40.2 0.0 collective-permute-start.7
  40.2 0.0 collective-permute-done.10.refs_3_
  40.2 1.1 collective-permute-start.17
  41.2 0.0 collective-permute-done.11.refs_4_
  41.2 0.7 collective-permute-start.14
  41.9 0.0 collective-permute-done.12.refs_5_
  41.9 0.1 collective-permute-start.15
  42.0 0.0 collective-permute-done.13.refs_6_
  42.0 0.4 collective-permute-start.16
  42.4 3.2 %collective-permute-done.17.refs_10_ = bf16[1,96,896]{2,1,0:T(8,128)(2,1)S(1)} collective-permute-done((bf16[1,96,896]{2,1,0:T(8,128)(2,1)S(1)}, bf16[1,96,896]{2,1,0:T(8,128)(2,1)S(1)}, u32[]{:S(2)}, u32[]{:S(2)}) %collective-permute-start.17) | collective-permute-done | bytes 172064 | tf_op jit(solution)/shard_map/ppermute | solution.py:235
  45.6 0.0 collective-permute-start.18
  45.6 0.7 convert_element_type.5
  46.3 0.6 broadcast_in_dim.27.mask
  46.9 1.0 pad_maximum_fusion.refs_0_
  47.9 0.0 collective-permute-done.18.refs_11_
  47.9 0.6 collective-permute-start.3
  48.5 0.0 collective-permute-done.7.refs_3_.refs_1_
  48.5 0.0 collective-permute-done.14.refs_7_
  48.5 0.0 collective-permute-done.15.refs_8_
  48.5 0.0 collective-permute-done.16.refs_9_
  48.5 22.8 %row_stats.3 = f32[3,512]{1,0:T(4,128)S(1)} custom-call(s32[73]{0:T(128)S(1)} %stack.32.info, s32[8,512]{1,0:T(8,128)S(1)} %broadcast_in_dim.26.limits, bf16[4752,3584]{1,0:T(8,128)(2,1)} %bitcast.16, bf16[3,96,896]{2,1,0:T(8,128)(2,1)S(1)} %constant_dynamic-update-slice_fusion.refs_2_.refs_0_, ...), custom_call_target="tpu_custom_call" | custom-call | flops 17439916032 | bytes 34062336 | tf_op jit(solution)/shard_map/row_stats/pallas_call | solution.py:139
  71.3 0.0 copy-start.1
  71.3 0.0 collective-permute-done.3.refs_1_
  71.3 14.2 %row_stats.2 = f32[3,256]{1,0:T(4,128)S(1)} custom-call(s32[37]{0:T(128)S(1)} %stack.31.info, s32[8,256]{1,0:T(8,128)S(1)} %broadcast_in_dim.25.limits, bf16[4752,3584]{1,0:T(8,128)(2,1)} %bitcast.17, bf16[4,96,896]{2,1,0:T(8,128)(2,1)S(1)} %pad_maximum_fusion.refs_0_, bf16[4,96,896]{2,1,0:T(8,128)(2,1)S(1)} %collective-permute-done.3.refs_1_, ...), custom_call_target="tpu_custom_call" | custom-call | flops 8719958016 | bytes 34062336 | tf_op jit(solution)/shard_map/row_stats/pallas_call | solution.py:139
  85.5 5.7 %all-gather.1.parts = f32[4,3,768]{2,1,0:T(4,128)} all-gather(f32[1,3,768]{2,1,0:T(4,128)S(1)} %maximum_bitcast_fusion), channel_id=2, replica_groups=mesh['seq'=8,'vocab'=4] {'vocab'}, dimensions={0}, use_global_device_ids=true | all-gather | bytes 46080 | tf_op jit(solution)/shard_map/all_gather | solution.py:355
  91.2 1.6 %combine.1 = f32[8,4,768]{2,1,0:T(4,128)} custom-call(s32[1]{0:T(128)} %bitcast.own, f32[4,3,768]{2,1,0:T(4,128)} %all-gather.1.parts, f32[1,768]{1,0:T(1,128)} %broadcast_in_dim.27.mask), custom_call_target="tpu_custom_call" | custom-call | tf_op jit(solution)/shard_map/combine/pallas_call | solution.py:191
  92.8 5.1 %all-to-all-start = ((f32[8,4,768]{2,1,0:T(4,128)}), f32[8,4,768]{2,1,0:T(4,128)S(1)}, u32[]{:S(2)}, u32[]{:S(2)}) async-start(f32[8,4,768]{2,1,0:T(4,128)} %combine.1), calls=%async_computation | async-start | bytes 196608 | tf_op jit(solution)/shard_map/all_to_all | solution.py:356
  98.0 0.0 copy-done.1
  98.0 0.6 broadcast_in_dim.28.owner
  98.6 0.6 broadcast_in_dim.29.place
  99.2 5.9 %all-to-all-done.parts = f32[8,4,768]{2,1,0:T(4,128)S(1)} async-done(((f32[8,4,768]{2,1,0:T(4,128)}), f32[8,4,768]{2,1,0:T(4,128)S(1)}, u32[]{:S(2)}, u32[]{:S(2)}) %all-to-all-start) | async-done | bytes 98336 | tf_op jit(solution)/shard_map/all_to_all | solution.py:356
  105.1 0.0 copy-start
  105.1 0.6 copy-done
  105.7 1.7 %finish.1 = (f32[1,96]{1,0:T(1,128)}, f32[1,1]{1,0:T(1,128)}) custom-call(s32[1]{0:T(128)} %bitcast.own, f32[8,4,768]{2,1,0:T(4,128)} %copy-done, s32[1,768]{1,0:T(1,128)} %broadcast_in_dim.28.owner, s32[1,768]{1,0:T(1,128)} %broadcast_in_dim.29.place), custom_call_target="tpu_custom_call" | custom-call | tf_op jit(solution)/shard_map/finish/pallas_call | solution.py:220
  (17 shorter events, 0.2 us)
Async XLA Ops:
  0.6 22.9 %collective-permute-start = (bf16[1,96,896]{2,1,0:T(8,128)(2,1)}, bf16[1,96,896]{2,1,0:T(8,128)(2,1)S(1)}, u32[]{:S(2)}, u32[]{:S(2)}) collective-permute-start(bf16[1,96,896]{2,1,0:T(8,128)(2,1)} %bitcast.18), channel_id=1, source_target_pairs={{0,2},{1,5},{2,0},{3,7},{4,6},{5,1},{6,4},{7,3},{8,10},{9,13},{10,... | collective-permute-start | bytes 516104 | tf_op jit(solution)/shard_map/ppermute | solution.py:235
  3.7 21.5 %collective-permute-start.1 = (bf16[1,96,896]{2,1,0:T(8,128)(2,1)}, bf16[1,96,896]{2,1,0:T(8,128)(2,1)S(1)}, u32[]{:S(2)}, u32[]{:S(2)}) collective-permute-start(bf16[1,96,896]{2,1,0:T(8,128)(2,1)} %bitcast.19), channel_id=1, source_target_pairs={{0,4},{1,3},{2,6},{3,1},{4,0},{5,7},{6,2},{7,5},{8,12},{9,11},{10,... | collective-permute-start | bytes 516104 | tf_op jit(solution)/shard_map/ppermute | solution.py:235
  5.2 8.1 %collective-permute-start.4 = (bf16[1,96,896]{2,1,0:T(8,128)(2,1)}, bf16[1,96,896]{2,1,0:T(8,128)(2,1)S(1)}, u32[]{:S(2)}, u32[]{:S(2)}) collective-permute-start(bf16[1,96,896]{2,1,0:T(8,128)(2,1)} %bitcast.20), channel_id=1, source_target_pairs={{0,8},{1,9},{2,10},{3,11},{4,12},{5,13},{6,14},{7,15},{8,0},{9,1},... | collective-permute-start | bytes 516104 | tf_op jit(solution)/shard_map/ppermute | solution.py:235
  6.8 15.7 %collective-permute-start.8 = (bf16[1,96,896]{2,1,0:T(8,128)(2,1)}, bf16[1,96,896]{2,1,0:T(8,128)(2,1)S(1)}, u32[]{:S(2)}, u32[]{:S(2)}) collective-permute-start(bf16[1,96,896]{2,1,0:T(8,128)(2,1)} %bitcast.21), channel_id=1, source_target_pairs={{0,16},{1,17},{2,18},{3,19},{4,20},{5,21},{6,22},{7,23},{8,24},{9,... | collective-permute-start | bytes 516104 | tf_op jit(solution)/shard_map/ppermute | solution.py:235
  9.3 13.6 %collective-permute-start.9 = (bf16[1,96,896]{2,1,0:T(8,128)(2,1)}, bf16[1,96,896]{2,1,0:T(8,128)(2,1)S(1)}, u32[]{:S(2)}, u32[]{:S(2)}) collective-permute-start(bf16[1,96,896]{2,1,0:T(8,128)(2,1)} %bitcast.22), channel_id=1, source_target_pairs={{0,24},{1,25},{2,26},{3,27},{4,28},{5,29},{6,30},{7,31},{8,16},{9,... | collective-permute-start | bytes 516104 | tf_op jit(solution)/shard_map/ppermute | solution.py:235
  13.2 13.4 %collective-permute-start.5 = (bf16[1,96,896]{2,1,0:T(8,128)(2,1)S(1)}, bf16[1,96,896]{2,1,0:T(8,128)(2,1)S(1)}, u32[]{:S(2)}, u32[]{:S(2)}) collective-permute-start(bf16[1,96,896]{2,1,0:T(8,128)(2,1)S(1)} %collective-permute-done.4), channel_id=1, source_target_pairs={{0,2},{1,5},{2,0},{3,7},{4,6},{5,1},{6,4},{7,3},{8,10},{9,13},{10,... | collective-permute-start | bytes 516104 | tf_op jit(solution)/shard_map/ppermute | solution.py:235
  22.4 8.6 %collective-permute-start.6 = (bf16[1,96,896]{2,1,0:T(8,128)(2,1)S(1)}, bf16[1,96,896]{2,1,0:T(8,128)(2,1)S(1)}, u32[]{:S(2)}, u32[]{:S(2)}) collective-permute-start(bf16[1,96,896]{2,1,0:T(8,128)(2,1)S(1)} %collective-permute-done.4), channel_id=1, source_target_pairs={{0,4},{1,3},{2,6},{3,1},{4,0},{5,7},{6,2},{7,5},{8,12},{9,11},{10,... | collective-permute-start | bytes 516104 | tf_op jit(solution)/shard_map/ppermute | solution.py:235
  23.0 17.2 %collective-permute-start.10 = (bf16[2,96,896]{2,1,0:T(8,128)(2,1)S(1)}, bf16[2,96,896]{2,1,0:T(8,128)(2,1)S(1)}, u32[]{:S(2)}, u32[]{:S(2)}) collective-permute-start(bf16[2,96,896]{2,1,0:T(8,128)(2,1)S(1)} %constant_dynamic-update-slice_fusion.3.refs_2_), channel_id=1, source_target_pairs={{0,2},{1,3},{2,0},{3,1},{4,6},{5,7},{6,4},{7,5},{8,10},{9,11},{10,... | collective-permute-start | bytes 1032200 | tf_op jit(solution)/shard_map/ppermute | solution.py:235
  23.6 17.7 %collective-permute-start.11 = (bf16[2,96,896]{2,1,0:T(8,128)(2,1)S(1)}, bf16[2,96,896]{2,1,0:T(8,128)(2,1)S(1)}, u32[]{:S(2)}, u32[]{:S(2)}) collective-permute-start(bf16[2,96,896]{2,1,0:T(8,128)(2,1)S(1)} %constant_dynamic-update-slice_fusion.3.refs_2_), channel_id=1, source_target_pairs={{0,4},{1,5},{2,6},{3,7},{4,0},{5,1},{6,2},{7,3},{8,12},{9,13},{10,... | collective-permute-start | bytes 1032200 | tf_op jit(solution)/shard_map/ppermute | solution.py:235
  25.1 16.8 %collective-permute-start.12 = (bf16[2,96,896]{2,1,0:T(8,128)(2,1)S(1)}, bf16[2,96,896]{2,1,0:T(8,128)(2,1)S(1)}, u32[]{:S(2)}, u32[]{:S(2)}) collective-permute-start(bf16[2,96,896]{2,1,0:T(8,128)(2,1)S(1)} %constant_dynamic-update-slice_fusion.3.refs_2_), channel_id=1, source_target_pairs={{0,6},{1,7},{2,4},{3,5},{4,2},{5,3},{6,0},{7,1},{8,14},{9,15},{10,... | collective-permute-start | bytes 1032200 | tf_op jit(solution)/shard_map/ppermute | solution.py:235
  26.6 15.4 %collective-permute-start.13 = (bf16[2,96,896]{2,1,0:T(8,128)(2,1)S(1)}, bf16[2,96,896]{2,1,0:T(8,128)(2,1)S(1)}, u32[]{:S(2)}, u32[]{:S(2)}) collective-permute-start(bf16[2,96,896]{2,1,0:T(8,128)(2,1)S(1)} %constant_dynamic-update-slice_fusion.3.refs_2_), channel_id=1, source_target_pairs={{0,1},{1,0},{2,3},{3,2},{4,5},{5,4},{6,7},{7,6},{8,9},{9,8},{10,11... | collective-permute-start | bytes 1032200 | tf_op jit(solution)/shard_map/ppermute | solution.py:235
  31.0 9.2 %collective-permute-start.2 = (bf16[1,96,896]{2,1,0:T(8,128)(2,1)S(1)}, bf16[1,96,896]{2,1,0:T(8,128)(2,1)S(1)}, u32[]{:S(2)}, u32[]{:S(2)}) collective-permute-start(bf16[1,96,896]{2,1,0:T(8,128)(2,1)S(1)} %collective-permute-done), channel_id=1, source_target_pairs={{0,4},{1,3},{2,6},{3,1},{4,0},{5,7},{6,2},{7,5},{8,12},{9,11},{10,... | collective-permute-start | bytes 516104 | tf_op jit(solution)/shard_map/ppermute | solution.py:235
  40.2 8.3 %collective-permute-start.7 = (bf16[3,96,896]{2,1,0:T(8,128)(2,1)S(1)}, bf16[3,96,896]{2,1,0:T(8,128)(2,1)S(1)}, u32[]{:S(2)}, u32[]{:S(2)}) collective-permute-start(bf16[3,96,896]{2,1,0:T(8,128)(2,1)S(1)} %constant_dynamic-update-slice_fusion.refs_2_.refs_0_), channel_id=1, source_target_pairs={{0,1},{1,0},{2,3},{3,2},{4,5},{5,4},{6,7},{7,6},{8,9},{9,8},{10,11... | collective-permute-start | bytes 1548296 | tf_op jit(solution)/shard_map/ppermute | solution.py:235
  40.2 5.4 %collective-permute-start.17 = (bf16[1,96,896]{2,1,0:T(8,128)(2,1)S(1)}, bf16[1,96,896]{2,1,0:T(8,128)(2,1)S(1)}, u32[]{:S(2)}, u32[]{:S(2)}) collective-permute-start(bf16[1,96,896]{2,1,0:T(8,128)(2,1)S(1)} %collective-permute-done.5), channel_id=1, source_target_pairs={{0,4},{1,3},{2,6},{3,1},{4,0},{5,7},{6,2},{7,5},{8,12},{9,11},{10,... | collective-permute-start | bytes 516104 | tf_op jit(solution)/shard_map/ppermute | solution.py:235
  41.2 7.2 %collective-permute-start.14 = (bf16[2,96,896]{2,1,0:T(8,128)(2,1)S(1)}, bf16[2,96,896]{2,1,0:T(8,128)(2,1)S(1)}, u32[]{:S(2)}, u32[]{:S(2)}) collective-permute-start(bf16[2,96,896]{2,1,0:T(8,128)(2,1)S(1)} %collective-permute-done.10.refs_3_), channel_id=1, source_target_pairs={{0,1},{1,0},{2,3},{3,2},{4,5},{5,4},{6,7},{7,6},{8,9},{9,8},{10,11... | collective-permute-start | bytes 1032200 | tf_op jit(solution)/shard_map/ppermute | solution.py:235
  41.9 6.6 %collective-permute-start.15 = (bf16[2,96,896]{2,1,0:T(8,128)(2,1)S(1)}, bf16[2,96,896]{2,1,0:T(8,128)(2,1)S(1)}, u32[]{:S(2)}, u32[]{:S(2)}) collective-permute-start(bf16[2,96,896]{2,1,0:T(8,128)(2,1)S(1)} %collective-permute-done.11.refs_4_), channel_id=1, source_target_pairs={{0,1},{1,0},{2,3},{3,2},{4,5},{5,4},{6,7},{7,6},{8,9},{9,8},{10,11... | collective-permute-start | bytes 1032200 | tf_op jit(solution)/shard_map/ppermute | solution.py:235
  42.0 6.5 %collective-permute-start.16 = (bf16[2,96,896]{2,1,0:T(8,128)(2,1)S(1)}, bf16[2,96,896]{2,1,0:T(8,128)(2,1)S(1)}, u32[]{:S(2)}, u32[]{:S(2)}) collective-permute-start(bf16[2,96,896]{2,1,0:T(8,128)(2,1)S(1)} %collective-permute-done.12.refs_5_), channel_id=1, source_target_pairs={{0,1},{1,0},{2,3},{3,2},{4,5},{5,4},{6,7},{7,6},{8,9},{9,8},{10,11... | collective-permute-start | bytes 1032200 | tf_op jit(solution)/shard_map/ppermute | solution.py:235
  45.6 2.3 %collective-permute-start.18 = (bf16[1,96,896]{2,1,0:T(8,128)(2,1)S(1)}, bf16[1,96,896]{2,1,0:T(8,128)(2,1)S(1)}, u32[]{:S(2)}, u32[]{:S(2)}) collective-permute-start(bf16[1,96,896]{2,1,0:T(8,128)(2,1)S(1)} %collective-permute-done.17.refs_10_), channel_id=1, source_target_pairs={{0,1},{1,0},{2,3},{3,2},{4,5},{5,4},{6,7},{7,6},{8,9},{9,8},{10,11... | collective-permute-start | bytes 516104 | tf_op jit(solution)/shard_map/ppermute | solution.py:235
  47.9 23.4 %collective-permute-start.3 = (bf16[4,96,896]{2,1,0:T(8,128)(2,1)S(1)}, bf16[4,96,896]{2,1,0:T(8,128)(2,1)S(1)}, u32[]{:S(2)}, u32[]{:S(2)}) collective-permute-start(bf16[4,96,896]{2,1,0:T(8,128)(2,1)S(1)} %pad_maximum_fusion.refs_0_), channel_id=1, source_target_pairs={{0,1},{1,0},{2,3},{3,2},{4,5},{5,4},{6,7},{7,6},{8,9},{9,8},{10,11... | collective-permute-start | bytes 2064392 | tf_op jit(solution)/shard_map/ppermute | solution.py:235
  71.3 26.7 %copy-start.1 = (s32[768]{0:T(1024)S(1)}, s32[768]{0:T(1024)}, u32[]{:S(2)}) copy-start(s32[768]{0:T(1024)} %param.7) | copy-start | bytes 9220
  92.8 12.3 %all-to-all-start = ((f32[8,4,768]{2,1,0:T(4,128)}), f32[8,4,768]{2,1,0:T(4,128)S(1)}, u32[]{:S(2)}, u32[]{:S(2)}) async-start(f32[8,4,768]{2,1,0:T(4,128)} %combine.1), calls=%async_computation | async-start | bytes 196608 | tf_op jit(solution)/shard_map/all_to_all | solution.py:356
  105.1 0.6 copy-start

commit v4 on v3

--- a/solution.py
+++ b/solution.py
@@ -167,9 +167,10 @@
     return top, jnp.sum(ratio * parts[:, 1], axis=0), jnp.sum(ratio * (parts[:, 2] + parts[:, 1] * drop), axis=0)
 
 
-def combine_kernel(groups, own, parts, mask, out):
-    tokens = parts.shape[2]
-    stats = list(merge(parts[...]))
+def combine_kernel(groups, own, mask, *refs):
+    parts, out = refs[:-1], refs[-1]
+    tokens = mask.shape[1]
+    stats = list(merge(jnp.stack([part[...] for part in parts])))
     stats = jnp.stack([*stats, stats[0]])
     lane = lax.broadcasted_iota(jnp.int32, stats.shape, 1)
     width = tokens // groups
@@ -187,14 +188,14 @@
 
 
 def combine(groups, own, parts, mask):
-    tokens = parts.shape[2]
+    tokens = mask.shape[1]
     return pl.pallas_call(
         functools.partial(combine_kernel, groups),
         out_shape=jax.ShapeDtypeStruct((groups, 4, tokens), jnp.float32),
-        in_specs=[pl.BlockSpec(memory_space=pltpu.SMEM)] + [pl.BlockSpec(memory_space=pltpu.VMEM)] * 2,
+        in_specs=[pl.BlockSpec(memory_space=pltpu.SMEM)] + [pl.BlockSpec(memory_space=pltpu.VMEM)] * (1 + len(parts)),
         out_specs=pl.BlockSpec(memory_space=pltpu.VMEM),
         name="combine",
-    )(own, parts, mask)
+    )(own, mask, *parts)
 
 
 def finish_kernel(own, parts, owner, place, entropy_out, mean_out):
@@ -352,7 +353,8 @@
 
     own = my_seq[None].astype(jnp.int32)
     mask = jnp.pad(loss_mask.astype(jnp.float32), (0, tokens - each))[None]
-    sent = combine(seq, own, lax.all_gather(stats, "vocab"), mask)
+    others = [permute(seq, vocab, stats, both(0, v)) for v in range(vocab - 1, 0, -1)]
+    sent = combine(seq, own, [stats, *others], mask)
     parts = lax.all_to_all(sent, "seq", 0, 0, tiled=True)
     entropy, mean = finish(own, parts, (positions // each)[None], (positions % each)[None], each)
     return entropy.reshape(each), mean.reshape(())

time: 108 us -> 107 us (level)
  blocking collectives: 5.67 us -> 0 us
  waiting for transfers between devices: 32.2 us -> 35.1 us
  starting transfers between devices: 21.9 us -> 23.5 us
    all_gather x1 -> x0, blocking collectives: 5.67 us -> none  [local(): sent = combine(seq, own, lax.all_gather(stats, 'vocab'), mask)]
    ppermute x19 -> x22, waiting for transfers between devices: 26.3 us -> 29.2 us  [permute(): return lax.ppermute(array, AXES, pairs)]
    ppermute x19 -> x22, starting transfers between devices: 16.8 us -> 18.4 us  [permute(): return lax.ppermute(array, AXES, pairs)]
  transfers between devices with their start and end apart: 20 -> 23, of which waited for: 6 -> 9; matrix products, arithmetic and copies ran while one was open for 5% -> 5% of each run, Pallas kernels for 21% -> 21%
where the time goes in v4:
time: 107 us; the launch traced here: 106 us
  Pallas kernels  40.3 us (38%)
  waiting for transfers between devices  35.1 us (33%)
  starting transfers between devices  23.5 us (22%)
  local copies, waits for them, and re-layouts  3.91 us (4%)
  other arithmetic  2.44 us (2%)
    pallas_call x2, Pallas kernels, row_stats(): pl.pallas_call(functools.partial(stats_kernel, half, steps, slots, paired...  37 us
    ppermute x22, waiting for transfers between devices, permute(): return lax.ppermute(array, AXES, pairs)  29.2 us
    ppermute x22, starting transfers between devices, permute(): return lax.ppermute(array, AXES, pairs)  18.4 us
    all_to_all x1, waiting for transfers between devices, local(): parts = lax.all_to_all(sent, 'seq', 0, 0, tiled=True)  5.93 us
    all_to_all x1, starting transfers between devices, local(): parts = lax.all_to_all(sent, 'seq', 0, 0, tiled=True)  5.11 us
  transfers between devices with their start and end apart: 23, of which 9 were waited for; matrix products, arithmetic and copies ran while one was open for 5% of the time, Pallas kernels for 21%

profile of v4, /device:TPU:0, one launch (start us, length us, event | category | flops | bytes accessed | tf_op | source)
XLA Modules:
  0.0 106.2 jit_solution(3149865687986802127)
XLA Ops:
  0.6 3.0 %collective-permute-start = (bf16[1,96,896]{2,1,0:T(8,128)(2,1)}, bf16[1,96,896]{2,1,0:T(8,128)(2,1)S(1)}, u32[]{:S(2)}, u32[]{:S(2)}) collective-permute-start(bf16[1,96,896]{2,1,0:T(8,128)(2,1)} %bitcast.16), channel_id=1, source_target_pairs={{0,2},{1,5},{2,0},{3,7},{4,6},{5,1},{6,4},{7,3},{8,10},{9,13},{10,... | collective-permute-start | bytes 516104 | tf_op jit(solution)/shard_map/ppermute | solution.py:236
  3.7 1.5 %collective-permute-start.1 = (bf16[1,96,896]{2,1,0:T(8,128)(2,1)}, bf16[1,96,896]{2,1,0:T(8,128)(2,1)S(1)}, u32[]{:S(2)}, u32[]{:S(2)}) collective-permute-start(bf16[1,96,896]{2,1,0:T(8,128)(2,1)} %bitcast.17), channel_id=1, source_target_pairs={{0,4},{1,3},{2,6},{3,1},{4,0},{5,7},{6,2},{7,5},{8,12},{9,11},{10,... | collective-permute-start | bytes 516104 | tf_op jit(solution)/shard_map/ppermute | solution.py:236
  5.2 1.6 %collective-permute-start.4 = (bf16[1,96,896]{2,1,0:T(8,128)(2,1)}, bf16[1,96,896]{2,1,0:T(8,128)(2,1)S(1)}, u32[]{:S(2)}, u32[]{:S(2)}) collective-permute-start(bf16[1,96,896]{2,1,0:T(8,128)(2,1)} %bitcast.18), channel_id=1, source_target_pairs={{0,8},{1,9},{2,10},{3,11},{4,12},{5,13},{6,14},{7,15},{8,0},{9,1},... | collective-permute-start | bytes 516104 | tf_op jit(solution)/shard_map/ppermute | solution.py:236
  6.8 2.6 %collective-permute-start.8 = (bf16[1,96,896]{2,1,0:T(8,128)(2,1)}, bf16[1,96,896]{2,1,0:T(8,128)(2,1)S(1)}, u32[]{:S(2)}, u32[]{:S(2)}) collective-permute-start(bf16[1,96,896]{2,1,0:T(8,128)(2,1)} %bitcast.19), channel_id=1, source_target_pairs={{0,16},{1,17},{2,18},{3,19},{4,20},{5,21},{6,22},{7,23},{8,24},{9,... | collective-permute-start | bytes 516104 | tf_op jit(solution)/shard_map/ppermute | solution.py:236
  9.3 0.2 collective-permute-start.9
  9.6 0.7 broadcast_minimum_fusion
  10.3 0.1 reshape.30
  10.4 0.1 reshape.31
  10.5 0.7 broadcast_select_fusion
  11.1 0.1 reshape.32
  11.2 0.1 rev.10
  11.3 0.1 reshape.33
  11.4 0.1 rev.11
  11.6 0.1 stack.31.info
  11.7 0.2 stack.32.info
  11.9 1.3 %collective-permute-done.4 = bf16[1,96,896]{2,1,0:T(8,128)(2,1)S(1)} collective-permute-done((bf16[1,96,896]{2,1,0:T(8,128)(2,1)}, bf16[1,96,896]{2,1,0:T(8,128)(2,1)S(1)}, u32[]{:S(2)}, u32[]{:S(2)}) %collective-permute-start.4) | collective-permute-done | bytes 172064 | tf_op jit(solution)/shard_map/ppermute | solution.py:236
  13.2 0.5 collective-permute-start.5
  13.8 8.6 %collective-permute-done.8 = bf16[1,96,896]{2,1,0:T(8,128)(2,1)S(1)} collective-permute-done((bf16[1,96,896]{2,1,0:T(8,128)(2,1)}, bf16[1,96,896]{2,1,0:T(8,128)(2,1)S(1)}, u32[]{:S(2)}, u32[]{:S(2)}) %collective-permute-start.8) | collective-permute-done | bytes 172064 | tf_op jit(solution)/shard_map/ppermute | solution.py:236
  22.4 0.5 collective-permute-start.6
  22.9 0.0 collective-permute-done.9
  23.0 0.6 collective-permute-start.10
  23.6 0.0 collective-permute-done
  23.6 1.5 %collective-permute-start.11 = (bf16[2,96,896]{2,1,0:T(8,128)(2,1)S(1)}, bf16[2,96,896]{2,1,0:T(8,128)(2,1)S(1)}, u32[]{:S(2)}, u32[]{:S(2)}) collective-permute-start(bf16[2,96,896]{2,1,0:T(8,128)(2,1)S(1)} %constant_dynamic-update-slice_fusion.3.refs_2_), channel_id=1, source_target_pairs={{0,4},{1,5},{2,6},{3,7},{4,0},{5,1},{6,2},{7,3},{8,12},{9,13},{10,... | collective-permute-start | bytes 1032200 | tf_op jit(solution)/shard_map/ppermute | solution.py:236
  25.1 0.0 collective-permute-done.1
  25.1 1.5 %collective-permute-start.12 = (bf16[2,96,896]{2,1,0:T(8,128)(2,1)S(1)}, bf16[2,96,896]{2,1,0:T(8,128)(2,1)S(1)}, u32[]{:S(2)}, u32[]{:S(2)}) collective-permute-start(bf16[2,96,896]{2,1,0:T(8,128)(2,1)S(1)} %constant_dynamic-update-slice_fusion.3.refs_2_), channel_id=1, source_target_pairs={{0,6},{1,7},{2,4},{3,5},{4,2},{5,3},{6,0},{7,1},{8,14},{9,15},{10,... | collective-permute-start | bytes 1032200 | tf_op jit(solution)/shard_map/ppermute | solution.py:236
  26.6 0.0 collective-permute-done.5
  26.6 0.0 collective-permute-start.13
  26.6 4.3 %collective-permute-done.6 = bf16[1,96,896]{2,1,0:T(8,128)(2,1)S(1)} collective-permute-done((bf16[1,96,896]{2,1,0:T(8,128)(2,1)S(1)}, bf16[1,96,896]{2,1,0:T(8,128)(2,1)S(1)}, u32[]{:S(2)}, u32[]{:S(2)}) %collective-permute-start.6) | collective-permute-done | bytes 172064 | tf_op jit(solution)/shard_map/ppermute | solution.py:236
  31.0 0.4 collective-permute-start.2
  31.4 8.8 %collective-permute-done.2 = bf16[1,96,896]{2,1,0:T(8,128)(2,1)S(1)} collective-permute-done((bf16[1,96,896]{2,1,0:T(8,128)(2,1)S(1)}, bf16[1,96,896]{2,1,0:T(8,128)(2,1)S(1)}, u32[]{:S(2)}, u32[]{:S(2)}) %collective-permute-start.2) | collective-permute-done | bytes 172064 | tf_op jit(solution)/shard_map/ppermute | solution.py:236
  40.2 0.0 collective-permute-start.7
  40.2 0.0 collective-permute-done.10.refs_3_
  40.2 1.1 collective-permute-start.17
  41.2 0.7 collective-permute-start.14
  41.9 0.0 collective-permute-done.12.refs_5_
  41.9 0.1 collective-permute-start.15
  42.0 0.4 collective-permute-start.16
  42.4 3.2 %collective-permute-done.17.refs_10_ = bf16[1,96,896]{2,1,0:T(8,128)(2,1)S(1)} collective-permute-done((bf16[1,96,896]{2,1,0:T(8,128)(2,1)S(1)}, bf16[1,96,896]{2,1,0:T(8,128)(2,1)S(1)}, u32[]{:S(2)}, u32[]{:S(2)}) %collective-permute-start.17) | collective-permute-done | bytes 172064 | tf_op jit(solution)/shard_map/ppermute | solution.py:236
  45.6 1.0 pad_maximum_fusion.refs_0_
  46.6 0.4 collective-permute-done.18.refs_11_
  47.0 0.2 collective-permute-start.3
  47.2 0.0 collective-permute-done.7.refs_3_.refs_1_
  47.2 0.0 collective-permute-done.16.refs_9_
  47.2 22.8 %row_stats.3 = f32[3,512]{1,0:T(4,128)S(1)} custom-call(s32[73]{0:T(128)S(1)} %stack.32.info, s32[8,512]{1,0:T(8,128)S(1)} %broadcast_in_dim.27.limits, bf16[4752,3584]{1,0:T(8,128)(2,1)} %bitcast.14, bf16[3,96,896]{2,1,0:T(8,128)(2,1)S(1)} %constant_dynamic-update-slice_fusion.refs_2_.refs_0_, ...), custom_call_target="tpu_custom_call" | custom-call | flops 17439916032 | bytes 34062336 | tf_op jit(solution)/shard_map/row_stats/pallas_call | solution.py:139
  70.0 0.0 copy-start.6
  70.1 0.0 copy-start.5
  70.1 0.0 collective-permute-done.3.refs_1_
  70.1 14.2 %row_stats.2 = f32[3,256]{1,0:T(4,128)S(1)} custom-call(s32[37]{0:T(128)S(1)} %stack.31.info, s32[8,256]{1,0:T(8,128)S(1)} %broadcast_in_dim.26.limits, bf16[4752,3584]{1,0:T(8,128)(2,1)} %bitcast.15, bf16[4,96,896]{2,1,0:T(8,128)(2,1)S(1)} %pad_maximum_fusion.refs_0_, bf16[4,96,896]{2,1,0:T(8,128)(2,1)S(1)} %collective-permute-done.3.refs_1_, ...), custom_call_target="tpu_custom_call" | custom-call | flops 8719958016 | bytes 34062336 | tf_op jit(solution)/shard_map/row_stats/pallas_call | solution.py:139
  84.3 1.5 %collective-permute-start.19 = (f32[3,768]{1,0:T(4,128)S(1)}, f32[3,768]{1,0:T(4,128)S(1)}, u32[]{:S(2)}, u32[]{:S(2)}) collective-permute-start(f32[3,768]{1,0:T(4,128)S(1)} %pad_maximum_fusion.1.refs_0_), channel_id=1, source_target_pairs={{0,3},{1,2},{2,1},{3,0},{4,7},{5,6},{6,5},{7,4},{8,11},{9,10},{10,... | collective-permute-start | bytes 27656 | tf_op jit(solution)/shard_map/ppermute | solution.py:236
  85.8 0.5 collective-permute-start.20
  86.3 0.0 collective-permute-start.21
  86.3 0.6 broadcast_in_dim.24.mask
  86.9 0.6 collective-permute-done.19.refs_1_
  87.5 2.0 %collective-permute-done.20.refs_2_ = f32[3,768]{1,0:T(4,128)S(1)} collective-permute-done((f32[3,768]{1,0:T(4,128)S(1)}, f32[3,768]{1,0:T(4,128)S(1)}, u32[]{:S(2)}, u32[]{:S(2)}) %collective-permute-start.20) | collective-permute-done | bytes 9248 | tf_op jit(solution)/shard_map/ppermute | solution.py:236
  89.5 0.0 collective-permute-done.21.refs_3_
  89.5 0.6 copy-done.3
  90.1 0.0 copy-done.4
  90.1 1.6 %combine.1 = f32[8,4,768]{2,1,0:T(4,128)} custom-call(s32[1]{0:T(128)} %bitcast.own, f32[1,768]{1,0:T(1,128)} %broadcast_in_dim.24.mask, f32[3,768]{1,0:T(4,128)} %copy-done.1, f32[3,768]{1,0:T(4,128)} %copy-done.2, f32[3,768]{1,0:T(4,128)} %copy-done.3, f32[3,768]{1,0:T(4,128)} %copy-done.4), custom_call_target="tpu_custom_call" | custom-call | tf_op jit(solution)/shard_map/combine/pallas_call | solution.py:192
  91.7 5.1 %all-to-all-start = ((f32[8,4,768]{2,1,0:T(4,128)}), f32[8,4,768]{2,1,0:T(4,128)S(1)}, u32[]{:S(2)}, u32[]{:S(2)}) async-start(f32[8,4,768]{2,1,0:T(4,128)} %combine.1), calls=%async_computation | async-start | bytes 196608 | tf_op jit(solution)/shard_map/all_to_all | solution.py:358
  96.8 0.6 broadcast_in_dim.28.owner
  97.4 0.6 broadcast_in_dim.29.place
  98.0 5.9 %all-to-all-done.parts = f32[8,4,768]{2,1,0:T(4,128)S(1)} async-done(((f32[8,4,768]{2,1,0:T(4,128)}), f32[8,4,768]{2,1,0:T(4,128)S(1)}, u32[]{:S(2)}, u32[]{:S(2)}) %all-to-all-start) | async-done | bytes 98336 | tf_op jit(solution)/shard_map/all_to_all | solution.py:358
  103.9 0.6 copy-done
  104.6 1.7 %finish.1 = (f32[1,96]{1,0:T(1,128)}, f32[1,1]{1,0:T(1,128)}) custom-call(s32[1]{0:T(128)} %bitcast.own, f32[8,4,768]{2,1,0:T(4,128)} %copy-done, s32[1,768]{1,0:T(1,128)} %broadcast_in_dim.28.owner, s32[1,768]{1,0:T(1,128)} %broadcast_in_dim.29.place), custom_call_target="tpu_custom_call" | custom-call | tf_op jit(solution)/shard_map/finish/pallas_call | solution.py:221
  (32 shorter events, 0.2 us)
Async XLA Ops:
  0.6 22.9 %collective-permute-start = (bf16[1,96,896]{2,1,0:T(8,128)(2,1)}, bf16[1,96,896]{2,1,0:T(8,128)(2,1)S(1)}, u32[]{:S(2)}, u32[]{:S(2)}) collective-permute-start(bf16[1,96,896]{2,1,0:T(8,128)(2,1)} %bitcast.16), channel_id=1, source_target_pairs={{0,2},{1,5},{2,0},{3,7},{4,6},{5,1},{6,4},{7,3},{8,10},{9,13},{10,... | collective-permute-start | bytes 516104 | tf_op jit(solution)/shard_map/ppermute | solution.py:236
  3.7 21.5 %collective-permute-start.1 = (bf16[1,96,896]{2,1,0:T(8,128)(2,1)}, bf16[1,96,896]{2,1,0:T(8,128)(2,1)S(1)}, u32[]{:S(2)}, u32[]{:S(2)}) collective-permute-start(bf16[1,96,896]{2,1,0:T(8,128)(2,1)} %bitcast.17), channel_id=1, source_target_pairs={{0,4},{1,3},{2,6},{3,1},{4,0},{5,7},{6,2},{7,5},{8,12},{9,11},{10,... | collective-permute-start | bytes 516104 | tf_op jit(solution)/shard_map/ppermute | solution.py:236
  5.2 8.1 %collective-permute-start.4 = (bf16[1,96,896]{2,1,0:T(8,128)(2,1)}, bf16[1,96,896]{2,1,0:T(8,128)(2,1)S(1)}, u32[]{:S(2)}, u32[]{:S(2)}) collective-permute-start(bf16[1,96,896]{2,1,0:T(8,128)(2,1)} %bitcast.18), channel_id=1, source_target_pairs={{0,8},{1,9},{2,10},{3,11},{4,12},{5,13},{6,14},{7,15},{8,0},{9,1},... | collective-permute-start | bytes 516104 | tf_op jit(solution)/shard_map/ppermute | solution.py:236
  6.8 15.7 %collective-permute-start.8 = (bf16[1,96,896]{2,1,0:T(8,128)(2,1)}, bf16[1,96,896]{2,1,0:T(8,128)(2,1)S(1)}, u32[]{:S(2)}, u32[]{:S(2)}) collective-permute-start(bf16[1,96,896]{2,1,0:T(8,128)(2,1)} %bitcast.19), channel_id=1, source_target_pairs={{0,16},{1,17},{2,18},{3,19},{4,20},{5,21},{6,22},{7,23},{8,24},{9,... | collective-permute-start | bytes 516104 | tf_op jit(solution)/shard_map/ppermute | solution.py:236
  9.3 13.6 %collective-permute-start.9 = (bf16[1,96,896]{2,1,0:T(8,128)(2,1)}, bf16[1,96,896]{2,1,0:T(8,128)(2,1)S(1)}, u32[]{:S(2)}, u32[]{:S(2)}) collective-permute-start(bf16[1,96,896]{2,1,0:T(8,128)(2,1)} %bitcast.20), channel_id=1, source_target_pairs={{0,24},{1,25},{2,26},{3,27},{4,28},{5,29},{6,30},{7,31},{8,16},{9,... | collective-permute-start | bytes 516104 | tf_op jit(solution)/shard_map/ppermute | solution.py:236
  13.2 13.4 %collective-permute-start.5 = (bf16[1,96,896]{2,1,0:T(8,128)(2,1)S(1)}, bf16[1,96,896]{2,1,0:T(8,128)(2,1)S(1)}, u32[]{:S(2)}, u32[]{:S(2)}) collective-permute-start(bf16[1,96,896]{2,1,0:T(8,128)(2,1)S(1)} %collective-permute-done.4), channel_id=1, source_target_pairs={{0,2},{1,5},{2,0},{3,7},{4,6},{5,1},{6,4},{7,3},{8,10},{9,13},{10,... | collective-permute-start | bytes 516104 | tf_op jit(solution)/shard_map/ppermute | solution.py:236
  22.4 8.6 %collective-permute-start.6 = (bf16[1,96,896]{2,1,0:T(8,128)(2,1)S(1)}, bf16[1,96,896]{2,1,0:T(8,128)(2,1)S(1)}, u32[]{:S(2)}, u32[]{:S(2)}) collective-permute-start(bf16[1,96,896]{2,1,0:T(8,128)(2,1)S(1)} %collective-permute-done.4), channel_id=1, source_target_pairs={{0,4},{1,3},{2,6},{3,1},{4,0},{5,7},{6,2},{7,5},{8,12},{9,11},{10,... | collective-permute-start | bytes 516104 | tf_op jit(solution)/shard_map/ppermute | solution.py:236
  23.0 17.2 %collective-permute-start.10 = (bf16[2,96,896]{2,1,0:T(8,128)(2,1)S(1)}, bf16[2,96,896]{2,1,0:T(8,128)(2,1)S(1)}, u32[]{:S(2)}, u32[]{:S(2)}) collective-permute-start(bf16[2,96,896]{2,1,0:T(8,128)(2,1)S(1)} %constant_dynamic-update-slice_fusion.3.refs_2_), channel_id=1, source_target_pairs={{0,2},{1,3},{2,0},{3,1},{4,6},{5,7},{6,4},{7,5},{8,10},{9,11},{10,... | collective-permute-start | bytes 1032200 | tf_op jit(solution)/shard_map/ppermute | solution.py:236
  23.6 17.7 %collective-permute-start.11 = (bf16[2,96,896]{2,1,0:T(8,128)(2,1)S(1)}, bf16[2,96,896]{2,1,0:T(8,128)(2,1)S(1)}, u32[]{:S(2)}, u32[]{:S(2)}) collective-permute-start(bf16[2,96,896]{2,1,0:T(8,128)(2,1)S(1)} %constant_dynamic-update-slice_fusion.3.refs_2_), channel_id=1, source_target_pairs={{0,4},{1,5},{2,6},{3,7},{4,0},{5,1},{6,2},{7,3},{8,12},{9,13},{10,... | collective-permute-start | bytes 1032200 | tf_op jit(solution)/shard_map/ppermute | solution.py:236
  25.1 16.8 %collective-permute-start.12 = (bf16[2,96,896]{2,1,0:T(8,128)(2,1)S(1)}, bf16[2,96,896]{2,1,0:T(8,128)(2,1)S(1)}, u32[]{:S(2)}, u32[]{:S(2)}) collective-permute-start(bf16[2,96,896]{2,1,0:T(8,128)(2,1)S(1)} %constant_dynamic-update-slice_fusion.3.refs_2_), channel_id=1, source_target_pairs={{0,6},{1,7},{2,4},{3,5},{4,2},{5,3},{6,0},{7,1},{8,14},{9,15},{10,... | collective-permute-start | bytes 1032200 | tf_op jit(solution)/shard_map/ppermute | solution.py:236
  26.6 15.4 %collective-permute-start.13 = (bf16[2,96,896]{2,1,0:T(8,128)(2,1)S(1)}, bf16[2,96,896]{2,1,0:T(8,128)(2,1)S(1)}, u32[]{:S(2)}, u32[]{:S(2)}) collective-permute-start(bf16[2,96,896]{2,1,0:T(8,128)(2,1)S(1)} %constant_dynamic-update-slice_fusion.3.refs_2_), channel_id=1, source_target_pairs={{0,1},{1,0},{2,3},{3,2},{4,5},{5,4},{6,7},{7,6},{8,9},{9,8},{10,11... | collective-permute-start | bytes 1032200 | tf_op jit(solution)/shard_map/ppermute | solution.py:236
  31.0 9.2 %collective-permute-start.2 = (bf16[1,96,896]{2,1,0:T(8,128)(2,1)S(1)}, bf16[1,96,896]{2,1,0:T(8,128)(2,1)S(1)}, u32[]{:S(2)}, u32[]{:S(2)}) collective-permute-start(bf16[1,96,896]{2,1,0:T(8,128)(2,1)S(1)} %collective-permute-done), channel_id=1, source_target_pairs={{0,4},{1,3},{2,6},{3,1},{4,0},{5,7},{6,2},{7,5},{8,12},{9,11},{10,... | collective-permute-start | bytes 516104 | tf_op jit(solution)/shard_map/ppermute | solution.py:236
  40.2 7.0 %collective-permute-start.7 = (bf16[3,96,896]{2,1,0:T(8,128)(2,1)S(1)}, bf16[3,96,896]{2,1,0:T(8,128)(2,1)S(1)}, u32[]{:S(2)}, u32[]{:S(2)}) collective-permute-start(bf16[3,96,896]{2,1,0:T(8,128)(2,1)S(1)} %constant_dynamic-update-slice_fusion.refs_2_.refs_0_), channel_id=1, source_target_pairs={{0,1},{1,0},{2,3},{3,2},{4,5},{5,4},{6,7},{7,6},{8,9},{9,8},{10,11... | collective-permute-start | bytes 1548296 | tf_op jit(solution)/shard_map/ppermute | solution.py:236
  40.2 5.4 %collective-permute-start.17 = (bf16[1,96,896]{2,1,0:T(8,128)(2,1)S(1)}, bf16[1,96,896]{2,1,0:T(8,128)(2,1)S(1)}, u32[]{:S(2)}, u32[]{:S(2)}) collective-permute-start(bf16[1,96,896]{2,1,0:T(8,128)(2,1)S(1)} %collective-permute-done.5), channel_id=1, source_target_pairs={{0,4},{1,3},{2,6},{3,1},{4,0},{5,7},{6,2},{7,5},{8,12},{9,11},{10,... | collective-permute-start | bytes 516104 | tf_op jit(solution)/shard_map/ppermute | solution.py:236
  41.2 6.0 %collective-permute-start.14 = (bf16[2,96,896]{2,1,0:T(8,128)(2,1)S(1)}, bf16[2,96,896]{2,1,0:T(8,128)(2,1)S(1)}, u32[]{:S(2)}, u32[]{:S(2)}) collective-permute-start(bf16[2,96,896]{2,1,0:T(8,128)(2,1)S(1)} %collective-permute-done.10.refs_3_), channel_id=1, source_target_pairs={{0,1},{1,0},{2,3},{3,2},{4,5},{5,4},{6,7},{7,6},{8,9},{9,8},{10,11... | collective-permute-start | bytes 1032200 | tf_op jit(solution)/shard_map/ppermute | solution.py:236
  41.9 5.3 %collective-permute-start.15 = (bf16[2,96,896]{2,1,0:T(8,128)(2,1)S(1)}, bf16[2,96,896]{2,1,0:T(8,128)(2,1)S(1)}, u32[]{:S(2)}, u32[]{:S(2)}) collective-permute-start(bf16[2,96,896]{2,1,0:T(8,128)(2,1)S(1)} %collective-permute-done.11.refs_4_), channel_id=1, source_target_pairs={{0,1},{1,0},{2,3},{3,2},{4,5},{5,4},{6,7},{7,6},{8,9},{9,8},{10,11... | collective-permute-start | bytes 1032200 | tf_op jit(solution)/shard_map/ppermute | solution.py:236
  42.0 5.2 %collective-permute-start.16 = (bf16[2,96,896]{2,1,0:T(8,128)(2,1)S(1)}, bf16[2,96,896]{2,1,0:T(8,128)(2,1)S(1)}, u32[]{:S(2)}, u32[]{:S(2)}) collective-permute-start(bf16[2,96,896]{2,1,0:T(8,128)(2,1)S(1)} %collective-permute-done.12.refs_5_), channel_id=1, source_target_pairs={{0,1},{1,0},{2,3},{3,2},{4,5},{5,4},{6,7},{7,6},{8,9},{9,8},{10,11... | collective-permute-start | bytes 1032200 | tf_op jit(solution)/shard_map/ppermute | solution.py:236
  45.6 1.4 %collective-permute-start.18 = (bf16[1,96,896]{2,1,0:T(8,128)(2,1)S(1)}, bf16[1,96,896]{2,1,0:T(8,128)(2,1)S(1)}, u32[]{:S(2)}, u32[]{:S(2)}) collective-permute-start(bf16[1,96,896]{2,1,0:T(8,128)(2,1)S(1)} %collective-permute-done.17.refs_10_), channel_id=1, source_target_pairs={{0,1},{1,0},{2,3},{3,2},{4,5},{5,4},{6,7},{7,6},{8,9},{9,8},{10,11... | collective-permute-start | bytes 516104 | tf_op jit(solution)/shard_map/ppermute | solution.py:236
  47.0 23.1 %collective-permute-start.3 = (bf16[4,96,896]{2,1,0:T(8,128)(2,1)S(1)}, bf16[4,96,896]{2,1,0:T(8,128)(2,1)S(1)}, u32[]{:S(2)}, u32[]{:S(2)}) collective-permute-start(bf16[4,96,896]{2,1,0:T(8,128)(2,1)S(1)} %pad_maximum_fusion.refs_0_), channel_id=1, source_target_pairs={{0,1},{1,0},{2,3},{3,2},{4,5},{5,4},{6,7},{7,6},{8,9},{9,8},{10,11... | collective-permute-start | bytes 2064392 | tf_op jit(solution)/shard_map/ppermute | solution.py:236
  70.0 16.3 %copy-start.6 = (s32[96]{0:T(128)S(1)}, s32[96]{0:T(128)}, u32[]{:S(2)}) copy-start(s32[96]{0:T(128)} %param.9) | copy-start | bytes 1156
  70.1 26.7 %copy-start.5 = (s32[768]{0:T(1024)S(1)}, s32[768]{0:T(1024)}, u32[]{:S(2)}) copy-start(s32[768]{0:T(1024)} %param.7) | copy-start | bytes 9220
  84.3 5.2 %copy-start.1 = (f32[3,768]{1,0:T(4,128)}, f32[3,768]{1,0:T(4,128)S(1)}, u32[]{:S(2)}) copy-start(f32[3,768]{1,0:T(4,128)S(1)} %pad_maximum_fusion.1.refs_0_) | copy-start | bytes 27652
  84.3 3.2 %collective-permute-start.19 = (f32[3,768]{1,0:T(4,128)S(1)}, f32[3,768]{1,0:T(4,128)S(1)}, u32[]{:S(2)}, u32[]{:S(2)}) collective-permute-start(f32[3,768]{1,0:T(4,128)S(1)} %pad_maximum_fusion.1.refs_0_), channel_id=1, source_target_pairs={{0,3},{1,2},{2,1},{3,0},{4,7},{5,6},{6,5},{7,4},{8,11},{9,10},{10,... | collective-permute-start | bytes 27656 | tf_op jit(solution)/shard_map/ppermute | solution.py:236
  85.8 3.7 %collective-permute-start.20 = (f32[3,768]{1,0:T(4,128)S(1)}, f32[3,768]{1,0:T(4,128)S(1)}, u32[]{:S(2)}, u32[]{:S(2)}) collective-permute-start(f32[3,768]{1,0:T(4,128)S(1)} %pad_maximum_fusion.1.refs_0_), channel_id=1, source_target_pairs={{0,2},{1,3},{2,0},{3,1},{4,6},{5,7},{6,4},{7,5},{8,10},{9,11},{10,... | collective-permute-start | bytes 27656 | tf_op jit(solution)/shard_map/ppermute | solution.py:236
  86.3 3.2 %collective-permute-start.21 = (f32[3,768]{1,0:T(4,128)S(1)}, f32[3,768]{1,0:T(4,128)S(1)}, u32[]{:S(2)}, u32[]{:S(2)}) collective-permute-start(f32[3,768]{1,0:T(4,128)S(1)} %pad_maximum_fusion.1.refs_0_), channel_id=1, source_target_pairs={{0,1},{1,0},{2,3},{3,2},{4,5},{5,4},{6,7},{7,6},{8,9},{9,8},{10,11... | collective-permute-start | bytes 27656 | tf_op jit(solution)/shard_map/ppermute | solution.py:236
  87.5 2.0 %copy-start.2 = (f32[3,768]{1,0:T(4,128)}, f32[3,768]{1,0:T(4,128)S(1)}, u32[]{:S(2)}) copy-start(f32[3,768]{1,0:T(4,128)S(1)} %collective-permute-done.19.refs_1_) | copy-start | bytes 27652
  89.5 0.6 copy-start.3
  89.5 0.6 copy-start.4
  91.7 12.2 %all-to-all-start = ((f32[8,4,768]{2,1,0:T(4,128)}), f32[8,4,768]{2,1,0:T(4,128)S(1)}, u32[]{:S(2)}, u32[]{:S(2)}) async-start(f32[8,4,768]{2,1,0:T(4,128)} %combine.1), calls=%async_computation | async-start | bytes 196608 | tf_op jit(solution)/shard_map/all_to_all | solution.py:358
  103.9 0.6 copy-start
